TPU v7x, 256 devices: a whole 4x4x8 slice. The times are simulated.
256 devices in a mesh: row: 8 (over x, z_lo), col: 8 (over z_hi, core), depth: 4 (over y).
Axes of the slice: x: 4, y: 4, z: 8 (z_hi: 4, z_lo: 2; z = z_hi * 2 + z_lo), core: 2. Of those that a mesh axis runs over, the one named last changes fastest.
Arguments:
- alignment_matrix: bfloat16 [128, 768, 256], P('depth', 'col'), may hold values from -6 to 6
- twin_linear_matrix: bfloat16 [256, 64], replicated, may hold values from -0.375 to 0.375
- final_matrix: bfloat16 [1024, 128], replicated, may hold values from -2 to 2
- final_offset: float32 [128], replicated, may hold values from -3 to 3
- adjoint_incoming: bfloat16 [768, 768, 128], P('row', ('col', 'depth')), may hold values from -6 to 6
Outputs:
- contact_delta: bfloat16 [768, 768, 128], P('row', ('col', 'depth'))
- alignment_adjoint: float32 [128, 768, 256], P('depth', 'col')
- grad_w_out: float32 [1024, 128], replicated
- grad_b_out: float32 [128], replicated
All inputs are finite; a program needn't handle non-finite values.
Results may differ from a plain program's by a relative error of at most 0.007.
Values may be sent and summed in bfloat16 or wider, within the bound.
No kernel may reach another device: no remote copies, remote signals or barrier semaphores. Data moves between devices by JAX's collectives and lax.ppermute only.
A program may use at most 128 MiB of HBM per device.

v0:
```python
import jax
import jax.numpy as jnp
from jax import lax
from jax.sharding import PartitionSpec as P

epsilon = 1e-05


def in_one(arrays, axis):
    vector, at, gathered = (jnp.concatenate([a.reshape(-1) for a in arrays]), 0, [])
    running = lax.psum(vector, axis)
    for a in arrays:
        gathered.append(running[at : at + a.size].reshape(a.shape))
        at += a.size
    return tuple(gathered)


def broadcast(shard, axis, root):
    return lax.dynamic_index_in_dim(lax.all_gather(shard, axis), root, 0, keepdims=False)


def copy_for_each(shard, axis):
    copies = jnp.broadcast_to(shard, (lax.axis_size(axis), *shard.shape))
    return lax.all_to_all(copies, axis, split_axis=0, concat_axis=0, tiled=True)


def of_everyone(shard, axis):
    everything = copy_for_each(shard, axis)
    return jnp.sum(everything, axis=0)


def standardize_channels(values):
    centre = jnp.mean(values, axis=-1, keepdims=True)
    spread = jnp.mean(jnp.square(values - centre), axis=-1, keepdims=True)
    return (values - centre) * lax.rsqrt(spread + epsilon)


def body(alignment_matrix, twin_linear_matrix, final_matrix, final_offset, adjoint_incoming):
    alignment_share, amino_share, discarded_item = alignment_matrix.shape
    latent_features = twin_linear_matrix.shape[1] // 2
    row_count = lax.axis_size("row")
    col_count = lax.axis_size("col")
    depth_count = lax.axis_size("depth")
    crop_length = amino_share * col_count
    block_i = crop_length // row_count
    quarter = amino_share // depth_count
    row_idx = lax.axis_index("row")
    col_idx = lax.axis_index("col")
    standardized_alignment, standardize_backprop = jax.vjp(
        standardize_channels, alignment_matrix.astype(jnp.float32)
    )
    normed = standardized_alignment.astype(jnp.bfloat16)
    panels = jnp.dot(normed, twin_linear_matrix, preferred_element_type=jnp.float32).astype(
        jnp.bfloat16
    )
    left_local = panels[..., :latent_features]
    right_local = panels[..., latent_features:]
    left_every = lax.all_gather(left_local, "col", axis=1, tiled=True)
    left_rows = lax.dynamic_slice_in_dim(left_every, row_idx * block_i, block_i, 1)
    left_seqs = lax.all_gather(left_rows, "depth", axis=0, tiled=True)
    right_seqs = lax.all_to_all(right_local, "depth", split_axis=1, concat_axis=0, tiled=True)
    seq_count = left_seqs.shape[0]
    summed = jnp.einsum(
        "sje,sic->jice", right_seqs, left_seqs, preferred_element_type=jnp.float32
    ).reshape(quarter, block_i, latent_features * latent_features)
    outer_mean = (summed / seq_count).astype(jnp.bfloat16)
    pair_cols = jnp.dot(outer_mean, final_matrix, preferred_element_type=jnp.float32) + final_offset
    contact_delta = jnp.transpose(pair_cols, (1, 0, 2)).astype(jnp.bfloat16)
    adjoint_kronecker = (
        jnp.einsum(
            "gtz,vz->gtv", adjoint_incoming, final_matrix, preferred_element_type=jnp.float32
        )
        / seq_count
    ).astype(jnp.bfloat16)
    grad_four = adjoint_kronecker.reshape(block_i, quarter, latent_features, latent_features)
    adjoint_leftside = jnp.einsum(
        "ijce,sje->sic", grad_four, right_seqs, preferred_element_type=jnp.float32
    )
    grad_right = jnp.einsum(
        "ijce,sic->sje", grad_four, left_seqs, preferred_element_type=jnp.float32
    )
    w_local = jnp.einsum(
        "jif,ijo->fo", outer_mean, adjoint_incoming, preferred_element_type=jnp.float32
    )
    b_local = jnp.sum(adjoint_incoming.astype(jnp.float32), axis=(0, 1))
    weight_gradient, bias_gradient = in_one((w_local, b_local), ("row", "col", "depth"))
    left_back, right_back = (
        lax.all_to_all(adjoint_leftside, "depth", split_axis=0, concat_axis=1, tiled=True),
        lax.all_to_all(grad_right, "depth", split_axis=0, concat_axis=1, tiled=True),
    )
    left_back = jnp.sum(
        left_back.reshape(alignment_share, depth_count, block_i, latent_features), axis=1
    )
    left_summed = lax.psum(left_back, "col")
    owner_row = col_idx * amino_share // block_i
    left_full = broadcast(left_summed.astype(jnp.bfloat16), "row", owner_row).astype(
        left_summed.dtype
    )
    right_full = of_everyone(right_back, "row")
    both_grads = jnp.concatenate([left_full, right_full], axis=-1)
    grad_panels = both_grads.astype(jnp.bfloat16)
    standardized_adjoint = jnp.einsum(
        "slk,mk->slm", grad_panels, twin_linear_matrix, preferred_element_type=jnp.float32
    )
    alignment_adjoint = standardize_backprop(standardized_adjoint)[0]
    return (
        contact_delta,
        alignment_adjoint,
        weight_gradient / crop_length,
        bias_gradient / crop_length,
    )


def solution(mesh):
    in_specs = (P("depth", "col", None), P(), P(), P(), P("row", ("col", "depth"), None))
    out_specs = (P("row", ("col", "depth"), None), P("depth", "col", None), P(), P())
    return jax.shard_map(body, mesh=mesh, in_specs=in_specs, out_specs=out_specs, check_vma=False)
```

profile of v0, /device:TPU:1, one launch (start us, length us, event | category | flops | bytes accessed | tf_op | source)
XLA Modules:
  0.0 472.1 jit_solution(5661845479301086679)
XLA Ops:
  8.1 2.1 convert_reduce_fusion
  10.2 2.4 fusion.8
  12.7 1.3 fusion.16
  14.1 2.0 copy.31
  16.2 1.2 copy.33
  17.4 1.4 reshape.73
  18.8 5.0 %all-to-all-start = ((bf16[4,2,12288]{2,1,0:T(2,128)(2,1)}), bf16[4,2,12288]{2,1,0:T(2,128)(2,1)S(1)}, u32[]{:S(2)}, u32[]{:S(2)}) async-start(bf16[4,2,12288]{2,1,0:T(2,128)(2,1)} %reshape.73), calls=%async_computation | async-start | bytes 393216 | tf_op jit(solution)/shard_map/all_to_all | solution.py:61
  23.8 3.5 multiply_convert_fusion.1
  27.3 8.5 %copy.39 = bf16[96,24,1024]{0,2,1:T(8,128)(2,1)} copy(bf16[96,24,1024]{2,1,0:T(8,128)(2,1)} %multiply_convert_fusion.1) | data formatting | bytes 9437184 | tf_op jit(solution)/shard_map/convert_element_type | solution.py:74
  35.8 0.4 reshape.74
  36.2 0.6 copy.56
  36.8 1.1 reshape.66
  37.9 5.1 %convolution_bitcast_fusion.1 = f32[128,96,32]{0,1,2:T(8,128)S(1)} fusion(bf16[96,24,32,32]{0,3,2,1:T(8,128)(2,1)} %bitcast.63, bf16[128,24,32,1]{0,2,1,3:T(8,128)(2,1)} %reshape.66), kind=kOutput, calls=%fused_computation.20 | convolution fusion | flops 603979776 | bytes 6488064 | tf_op jit(solution)/shard_map/ijce,sje->sic/dot_general | solution.py:76
  43.0 1.9 copy.41
  44.9 4.8 %all-to-all-start.1 = ((f32[128,96,32]{1,2,0:T(8,128)}), f32[128,96,32]{1,2,0:T(8,128)}, u32[]{:S(2)}, u32[]{:S(2)}) async-start(f32[128,96,32]{1,2,0:T(8,128)} %copy.41), calls=%async_computation.1 | async-start | bytes 4194304 | tf_op jit(solution)/shard_map/all_to_all | solution.py:88
  50.0 24.5 %all-to-all-done.1 = f32[128,96,32]{1,2,0:T(8,128)} async-done(((f32[128,96,32]{1,2,0:T(8,128)}), f32[128,96,32]{1,2,0:T(8,128)}, u32[]{:S(2)}, u32[]{:S(2)}) %all-to-all-start.1) | async-done | bytes 1572896 | tf_op jit(solution)/shard_map/all_to_all | solution.py:88
  74.6 2.7 reduce_sum.82
  77.3 13.4 %all-gather.4.cloned.1.call-done = bf16[32,768,32]{2,0,1:T(8,128)(2,1)} async-done(((bf16[32,96,32]{2,0,1:T(8,128)(2,1)}), bf16[32,768,32]{2,0,1:T(8,128)(2,1)}) %all-gather.4.cloned.1.call-update) | async-done | bytes 1572880 | tf_op jit(solution)/shard_map/all_gather | solution.py:58
  90.6 1.2 constant_dynamic-slice_fusion
  91.8 0.8 copy.32
  92.6 13.8 %all_gather.13 = bf16[128,96,32]{1,2,0:T(8,128)(2,1)S(1)} all-gather(bf16[32,96,32]{1,2,0:T(8,128)(2,1)S(1)} %copy.32), channel_id=1, replica_groups=mesh['row'=8,'col'=8,'depth'=4] {'depth'}, dimensions={0}, use_global_device_ids=true | all-gather | bytes 983040 | tf_op jit(solution)/shard_map/all_gather | solution.py:60
  106.4 5.0 %convolution_bitcast_fusion.2 = f32[128,24,32]{0,2,1:T(8,128)S(1)} fusion(bf16[96,24,32,32]{0,3,2,1:T(8,128)(2,1)} %bitcast.64, bf16[128,96,32]{1,2,0:T(8,128)(2,1)S(1)} %all_gather.13), kind=kOutput, calls=%fused_computation.25 | convolution fusion | flops 603979776 | bytes 5898240 | tf_op jit(solution)/shard_map/ijce,sic->sje/dot_general | solution.py:79
  111.4 2.4 copy.48
  113.9 1.6 copy.43
  115.5 2.8 reshape.75
  118.3 3.5 all-to-all-start.2
  121.8 9.1 %fusion = bf16[24,96,32,32]{3,2,0,1:T(8,128)(2,1)} fusion(bf16[128,96,32,1]{0,2,3,1:T(8,128)(2,1)S(1)} %copy.48, bf16[128,24,32,1]{0,2,1,3:T(8,128)(2,1)S(1)} %copy-done.7), kind=kOutput, calls=%fused_computation.1 | convolution fusion | flops 608698368 | bytes 5701632 | tf_op jit(solution)/shard_map/sje,sic->jice/dot_general | solution.py:63
  130.9 20.1 %copy.37 = bf16[24,96,32,32]{1,3,2,0:T(8,128)(2,1)} copy(bf16[24,96,32,32]{3,2,0,1:T(8,128)(2,1)} %fusion) | data formatting | bytes 9437184 | tf_op jit(solution)/shard_map/convert_element_type | solution.py:66
  151.0 0.5 broadcast.58
  151.5 2.5 reduce.2
  154.0 1.5 reshape.76
  155.5 1.8 copy.44
  157.4 2.4 all_to_all.47
  159.8 2.5 broadcast_in_dim.4
  162.3 4.7 all-to-all-start.3
  167.3 4.3 convolution_bitcast_fusion
  171.6 0.8 pad_maximum_fusion
  172.6 66.0 %all-reduce.4 = bf16[32,96,32]{1,2,0:T(8,128)(2,1)} all-reduce(f32[32,96,32]{1,2,0:T(8,128)S(1)} %copy-done.6), channel_id=1, replica_groups=mesh['row'=8,'col'=8,'depth'=4] {'col'}, use_global_device_ids=true, to_apply=%region_3.0 | all-reduce | flops 98304 | bytes 589824 | tf_op jit(solution)/shard_map/psum | solution.py:94
  238.7 4.6 fusion.19
  243.3 1.0 copy.47
  244.3 205.4 %all-reduce.3.cloned.1.call-done = f32[131200]{0:T(1024)} async-done(((f32[131200]{0:T(1024)}), f32[131200]{0:T(1024)}) %all-reduce.3.cloned.1.call-update) | async-done | bytes 524816 | tf_op jit(solution)/shard_map/psum | solution.py:11
  449.8 1.2 slice_multiply_fusion.1
  450.9 1.9 fusion.23
  452.8 1.0 dynamic-slice_bitcast_fusion
  453.8 2.8 reduce_sum.83
  456.6 3.2 multiply_reduce_fusion
  459.9 1.6 fusion.5
  461.5 3.2 fusion.7
  (36 shorter events, 0.9 us)
Async XLA Ops:
  8.0 15.8 %copy-start = (bf16[1024,128]{1,0:T(8,128)(2,1)S(1)}, bf16[1024,128]{1,0:T(8,128)(2,1)}, u32[]{:S(2)}) copy-start(bf16[1024,128]{1,0:T(8,128)(2,1)} %param.7) | copy-start | bytes 786436
  8.0 4.7 copy-start.1
  8.0 4.7 copy-start.8
  8.0 82.6 %all-gather.4.cloned.1.call-start = ((), (), s32[]{:S(2)}) async-start(), calls=%async_computation.4 | async-start | bytes 7077888 | tf_op jit(solution)/shard_map/all_gather | solution.py:58
  14.1 9.8 %copy-start.3 = (bf16[96,24,128]{2,1,0:T(8,128)(2,1)S(1)}, bf16[96,24,128]{2,1,0:T(8,128)(2,1)}, u32[]{:S(2)}) copy-start(bf16[96,24,128]{2,1,0:T(8,128)(2,1)} %param.9) | copy-start | bytes 1769476
  18.8 17.0 %all-to-all-start = ((bf16[4,2,12288]{2,1,0:T(2,128)(2,1)}), bf16[4,2,12288]{2,1,0:T(2,128)(2,1)S(1)}, u32[]{:S(2)}, u32[]{:S(2)}) async-start(bf16[4,2,12288]{2,1,0:T(2,128)(2,1)} %reshape.73), calls=%async_computation | async-start | bytes 393216 | tf_op jit(solution)/shard_map/all_to_all | solution.py:61
  44.9 4.8 %copy-start.4 = (bf16[96,24,128]{2,1,0:T(8,128)(2,1)S(1)}, bf16[96,24,128]{2,1,0:T(8,128)(2,1)}, u32[]{:S(2)}) copy-start(bf16[96,24,128]{2,1,0:T(8,128)(2,1)} %param.9) | copy-start | bytes 1769476
  44.9 29.7 %all-to-all-start.1 = ((f32[128,96,32]{1,2,0:T(8,128)}), f32[128,96,32]{1,2,0:T(8,128)}, u32[]{:S(2)}, u32[]{:S(2)}) async-start(f32[128,96,32]{1,2,0:T(8,128)} %copy.41), calls=%async_computation.1 | async-start | bytes 4194304 | tf_op jit(solution)/shard_map/all_to_all | solution.py:88
  106.4 5.0 %copy-start.2 = (bf16[128,96,32]{1,2,0:T(8,128)(2,1)}, bf16[128,96,32]{1,2,0:T(8,128)(2,1)S(1)}, u32[]{:S(2)}) copy-start(bf16[128,96,32]{1,2,0:T(8,128)(2,1)S(1)} %all_gather.13) | copy-start | bytes 2359300
  111.4 10.4 %copy-start.7 = (bf16[128,24,32,1]{0,2,1,3:T(8,128)(2,1)S(1)}, bf16[128,24,32,1]{0,2,1,3:T(8,128)(2,1)}, u32[]{:S(2)}) copy-start(bf16[128,24,32,1]{0,2,1,3:T(8,128)(2,1)} %reshape.66) | copy-start | bytes 589828
  118.3 32.7 %all-to-all-start.2 = ((f32[4,1,24576]{2,1,0:T(1,128)}), f32[4,1,24576]{2,1,0:T(1,128)S(1)}, u32[]{:S(2)}, u32[]{:S(2)}) async-start(f32[4,1,24576]{2,1,0:T(1,128)} %reshape.75), calls=%async_computation.2 | async-start | bytes 786432 | tf_op jit(solution)/shard_map/all_to_all | solution.py:89
  162.3 5.0 %copy-start.5 = (bf16[96,24,128]{2,1,0:T(8,128)(2,1)S(1)}, bf16[96,24,128]{2,1,0:T(8,128)(2,1)}, u32[]{:S(2)}) copy-start(bf16[96,24,128]{2,1,0:T(8,128)(2,1)} %param.9) | copy-start | bytes 1769476
  162.3 291.5 %all-to-all-start.3 = ((f32[8,32,96,32]{2,3,1,0:T(8,128)}), f32[8,32,96,32]{2,3,1,0:T(8,128)}, u32[]{:S(2)}, u32[]{:S(2)}) async-start(f32[8,32,96,32]{2,3,1,0:T(8,128)} %broadcast_in_dim.4), calls=%async_computation.3 | async-start | bytes 8388608 | tf_op jit(solution)/shard_map/all_to_all | solution.py:24
  167.0 282.8 %all-reduce.3.cloned.1.call-start = ((), (), s32[]{:S(2)}) async-start(), calls=%async_computation.5 | async-start | bytes 1056768 | tf_op jit(solution)/shard_map/psum | solution.py:11
  167.3 5.3 %copy-start.6 = (f32[32,96,32]{1,2,0:T(8,128)S(1)}, f32[32,96,32]{1,2,0:T(8,128)}, u32[]{:S(2)}) copy-start(f32[32,96,32]{1,2,0:T(8,128)} %reduce_sum.82) | copy-start | bytes 1179652
  167.3 71.4 %copy-start.9 = (f32[128]{0:T(128)S(1)}, f32[128]{0:T(128)}, u32[]{:S(2)}) copy-start(f32[128]{0:T(128)} %param.8) | copy-start | bytes 1540
  172.5 280.3 %all-gather.6.cloned.1.call-start = ((), (), s32[]{:S(2)}) async-start(), calls=%async_computation.6 | async-start | bytes 2359296 | tf_op jit(solution)/shard_map/all_gather | solution.py:19
Sparse Core Ops, SparseCore 0:
  16.3 74.2 all-gather.3
  173.9 275.8 all-reduce.2
Sparse Core Ops, SparseCore 1:
  238.7 60.2 all-gather.5
where the time goes:
time: 474 us; the launch traced here: 472 us
  waiting for transfers between devices  243 us (51%)
  blocking collectives  79.8 us (17%)
  local copies, waits for them, and re-layouts  57 us (12%)
  matrix products  36.2 us (8%)
  other arithmetic  21.6 us (5%)
  starting transfers between devices  18.3 us (4%)
  between operations  15.8 us (3%)
    psum x1, waiting for transfers between devices, in_one(): running = lax.psum(vector, axis)  205 us
    psum x1, blocking collectives, body(): left_summed = lax.psum(left_back, 'col')  66 us
    all_to_all x1, waiting for transfers between devices, body(): lax.all_to_all(adjoint_leftside, 'depth', split_axis=0, concat_axis=1, ti...  24.5 us
    convert_element_type x1, local copies, waits for them, and re-layouts, body(): outer_mean = (summed / seq_count).astype(jnp.bfloat16)  20.1 us
    all_gather x1, blocking collectives, body(): left_seqs = lax.all_gather(left_rows, 'depth', axis=0, tiled=True)  13.8 us
    all_gather x1, waiting for transfers between devices, body(): left_every = lax.all_gather(left_local, 'col', axis=1, tiled=True)  13.4 us
  transfers between devices with their start and end apart: 7, of which 3 were waited for; matrix products, arithmetic and copies ran while one was open for 15% of the time, Pallas kernels for 0%

commit v1 on v0

v1 whole, which is shorter than its diff:
```python
import jax
import jax.numpy as jnp
from jax import lax
from jax.experimental import pallas as pl
from jax.experimental.pallas import tpu as pltpu
from jax.sharding import PartitionSpec as P


epsilon = 1e-05
BF, F32 = jnp.bfloat16, jnp.float32
PLANE = ("row", "col")
TN = (((0,), (0,)), ((), ()))
NT = (((1,), (1,)), ((), ()))


def lane_mean(values):
    share = jnp.full((values.shape[-1], 128), 1.0 / values.shape[-1], BF)
    high = values.astype(BF)
    mean = jnp.dot(high, share, preferred_element_type=F32)
    if values.dtype == F32:
        low = (values - high.astype(F32)).astype(BF)
        mean = mean + jnp.dot(low, share, preferred_element_type=F32)
    return jnp.concatenate([mean, mean], axis=-1)


def standardized(rows):
    centred = rows.astype(F32) - lane_mean(rows)
    factor = lax.rsqrt(lane_mean(jnp.square(centred)) + epsilon)
    return centred * factor, factor


def panels_kernel(align_ref, weights_ref, left_ref, right_ref):
    share, amino, width = align_ref.shape
    latent = weights_ref.shape[0] // 2
    left_w, right_w = weights_ref[:latent], weights_ref[latent:]
    normed, _ = standardized(align_ref[...].reshape(share * amino, width))
    normed = normed.astype(BF)
    right = lax.dot_general(normed, right_w, NT, preferred_element_type=F32)
    right_ref[...] = right.astype(BF).reshape(right_ref.shape)
    for s in range(share):
        rows = normed[s * amino : (s + 1) * amino]
        left_ref[s] = lax.dot_general(left_w, rows, NT, preferred_element_type=F32).astype(BF)


def panels_of(align, weights):
    share, amino, width = align.shape
    latent = weights.shape[0] // 2
    whole = pl.BlockSpec((2 * latent, width), lambda g: (0, 0))
    return pl.pallas_call(
        panels_kernel,
        grid=(share // 8,),
        in_specs=[pl.BlockSpec((8, amino, width), lambda g: (g, 0, 0)), whole],
        out_specs=[
            pl.BlockSpec((8, latent, amino), lambda g: (g, 0, 0)),
            pl.BlockSpec((8, amino, latent), lambda g: (g, 0, 0)),
        ],
        out_shape=[
            jax.ShapeDtypeStruct((share, latent, amino), BF),
            jax.ShapeDtypeStruct((share, amino, latent), BF),
        ],
        name="panels",
    )(align, weights)


def align_kernel(align_ref, left_ref, right_ref, weights_ref, out_ref):
    share, amino, width = align_ref.shape
    latent = weights_ref.shape[0] // 2
    left_w, right_w = weights_ref[:latent], weights_ref[latent:]
    normed, factor = standardized(align_ref[...].reshape(share * amino, width))
    grad = jnp.concatenate([lax.dot_general(left_ref[s], left_w, TN, preferred_element_type=F32) for s in range(share)])
    right = right_ref[...].reshape(share * amino, latent)
    grad = grad + jnp.dot(right, right_w, preferred_element_type=F32)
    result = factor * (grad - lane_mean(grad) - normed * lane_mean(grad * normed))
    out_ref[...] = result.reshape(out_ref.shape)


def align_of(align, left_grad, right_grad, weights):
    share, amino, width = align.shape
    latent = weights.shape[0] // 2
    whole = pl.BlockSpec((2 * latent, width), lambda g: (0, 0))
    return pl.pallas_call(
        align_kernel,
        grid=(share // 8,),
        in_specs=[
            pl.BlockSpec((8, amino, width), lambda g: (g, 0, 0)),
            pl.BlockSpec((8, latent, amino), lambda g: (g, 0, 0)),
            pl.BlockSpec((8, amino, latent), lambda g: (g, 0, 0)),
            whole,
        ],
        out_specs=pl.BlockSpec((8, amino, width), lambda g: (g, 0, 0)),
        out_shape=jax.ShapeDtypeStruct(align.shape, F32),
        name="align",
    )(align, left_grad, right_grad, weights)


def swap_blocks(tiles):
    t0, t1, t2, t3 = tiles
    lane = lax.broadcasted_iota(jnp.int32, t0.shape, 1)
    half, quarter = (lane & 64) == 0, (lane & 32) == 0
    a0, a2 = jnp.where(half, t0, pltpu.roll(t2, 64, 1)), jnp.where(half, pltpu.roll(t0, 64, 1), t2)
    a1, a3 = jnp.where(half, t1, pltpu.roll(t3, 64, 1)), jnp.where(half, pltpu.roll(t1, 64, 1), t3)
    return (
        jnp.where(quarter, a0, pltpu.roll(a1, 32, 1)),
        jnp.where(quarter, pltpu.roll(a0, 96, 1), a1),
        jnp.where(quarter, a2, pltpu.roll(a3, 32, 1)),
        jnp.where(quarter, pltpu.roll(a2, 96, 1), a3),
    )


def grad_outer_kernel(scale, adj_ref, final_ref, right_ref, outer_ref, left_ref):
    quarter, block_i, width = adj_ref.shape
    final = final_ref[...]
    for four in range(quarter // 4):
        adj = adj_ref[four * 4 : (four + 1) * 4].reshape(4 * block_i, width)
        g = lax.dot_general(adj, final, NT, preferred_element_type=F32) * scale
        tiles = [g[j * block_i : (j + 1) * block_i] for j in range(4)]
        for c, tile in enumerate(swap_blocks(tiles)):
            outer_ref[c * block_i : (c + 1) * block_i, four * 128 : (four + 1) * 128] = tile.astype(BF)
    left_ref[...] = lax.dot_general(right_ref[...], outer_ref[...], NT, preferred_element_type=F32).astype(BF)


def grad_outer_of(adj, final, right, scale):
    _, block_i, width = adj.shape
    seqs, lanes = right.shape
    groups = final.shape[0] // 128
    return pl.pallas_call(
        lambda *refs: grad_outer_kernel(scale, *refs),
        grid=(groups,),
        in_specs=[
            pl.BlockSpec(adj.shape, lambda g: (0, 0, 0)),
            pl.BlockSpec((128, width), lambda g: (g, 0)),
            pl.BlockSpec(right.shape, lambda g: (0, 0)),
        ],
        out_specs=[
            pl.BlockSpec((4 * block_i, lanes), lambda g: (g, 0)),
            pl.BlockSpec((seqs, 4 * block_i), lambda g: (0, g)),
        ],
        out_shape=[
            jax.ShapeDtypeStruct((groups * 4 * block_i, lanes), BF),
            jax.ShapeDtypeStruct((seqs, groups * 4 * block_i), BF),
        ],
        name="grad_outer",
    )(adj, final, right)


def outer_kernel(scale, left_ref, right_ref, adj_ref, final_ref, offset_ref, pair_ref, weight_ref, outer_ref):
    step = pl.program_id(0)
    quarter, block_i, width = adj_ref.shape
    column = pl.ds(pl.multiple_of(step * 128, 128), 128)
    left = left_ref[...]
    for pair in range(quarter // 8):
        o = lax.dot_general(left, right_ref[:, pair * 256 : (pair + 1) * 256], TN, preferred_element_type=F32) * scale
        for part in range(2):
            tiles = [o[c * block_i : (c + 1) * block_i, part * 128 : (part + 1) * 128] for c in range(4)]
            for j, tile in enumerate(swap_blocks(tiles)):
                at = ((pair * 2 + part) * 4 + j) * block_i
                outer_ref[at : at + block_i, column] = tile.astype(BF)

    @pl.when(step == pl.num_programs(0) - 1)
    def _():
        weight = None
        for pair in range(quarter // 8):
            rows = slice(pair * 8 * block_i, (pair + 1) * 8 * block_i)
            outer = outer_ref[rows, :]
            adj = adj_ref[pair * 8 : (pair + 1) * 8].reshape(8 * block_i, width)
            pairs = jnp.dot(outer, final_ref[...], preferred_element_type=F32) + offset_ref[...]
            pair_ref[pair * 8 : (pair + 1) * 8] = pairs.astype(BF).reshape(8, block_i, width)
            part = lax.dot_general(adj, outer, TN, preferred_element_type=F32)
            weight = part if weight is None else weight + part
        weight_ref[...] = weight.T.astype(BF)


def outer_of(left, right, adj, final, offset, scale):
    quarter, block_i, width = adj.shape
    seqs = left.shape[0]
    whole = lambda shape: pl.BlockSpec(shape, lambda g: (0,) * len(shape))
    return pl.pallas_call(
        lambda *refs: outer_kernel(scale, *refs),
        grid=(left.shape[1] // (4 * block_i),),
        in_specs=[
            pl.BlockSpec((seqs, 4 * block_i), lambda g: (0, g)),
            whole(right.shape),
            whole(adj.shape),
            whole(final.shape),
            whole((1, width)),
        ],
        out_specs=[whole(adj.shape), whole(final.shape)],
        out_shape=[jax.ShapeDtypeStruct(adj.shape, BF), jax.ShapeDtypeStruct(final.shape, BF)],
        scratch_shapes=[pltpu.VMEM((quarter * block_i, final.shape[0]), BF)],
        name="outer",
    )(left, right, adj, final, offset.reshape(1, width))


def shifted(value, axis, by):
    n = lax.axis_size(axis)
    return lax.ppermute(value, axis, [(q, (q + by) % n) for q in range(n)])


def crossings():
    pairs = []
    for row in range(8):
        for col in range(8):
            source_row = ((col // 2 + row // 2) % 4) * 2 + col % 2
            pairs.append((source_row * 8 + row, row * 8 + col))
    return pairs


def exchange(pieces, axis):
    return lax.all_to_all(pieces, axis, split_axis=0, concat_axis=0, tiled=True)


def copies(piece, n):
    return jnp.broadcast_to(piece[None], (n, *piece.shape))


def step(alignment_matrix, twin_linear_matrix, final_matrix, final_offset, adjoint_incoming):
    share, amino, _ = alignment_matrix.shape
    latent = twin_linear_matrix.shape[1] // 2
    depth_count = lax.axis_size("depth")
    row_count = lax.axis_size("row")
    plane_count = row_count * lax.axis_size("col")
    crop_length = amino * lax.axis_size("col")
    _, quarter, width = adjoint_incoming.shape
    kron = final_matrix.shape[0]
    seq_count = share * depth_count
    there = crossings()
    back = [(b, a) for a, b in there]

    weights_t = twin_linear_matrix.T
    left_own, right_own = panels_of(alignment_matrix, weights_t)
    left_mine = lax.ppermute(left_own.reshape(share, latent * amino), PLANE, there)
    right_own = right_own.reshape(share, depth_count, quarter * latent).transpose(1, 0, 2)
    right = exchange(right_own, "depth").reshape(seq_count, quarter * latent)

    adj = jnp.transpose(adjoint_incoming, (1, 0, 2))
    adj, right, left_mine = lax.optimization_barrier((adj, right, left_mine))
    left = exchange(copies(left_mine, depth_count), "depth").reshape(seq_count, latent * amino)
    grad_outer, grad_left = grad_outer_of(adj, final_matrix, right, 1.0 / seq_count)
    grad_right = lax.dot_general(left, grad_outer, (((1,), (0,)), ((), ())), preferred_element_type=F32).astype(BF)
    grads = jnp.concatenate([grad_left, grad_right], axis=-1).reshape(depth_count, share, -1)
    grads = exchange(grads, "depth")
    pair_t, weight = outer_of(left, right, adj, final_matrix, final_offset, 1.0 / seq_count)
    contact_delta = jnp.transpose(pair_t, (1, 0, 2))

    left_sum = jnp.sum(grads[..., : latent * amino].astype(F32), axis=0).astype(BF)
    weight, left_sum = lax.optimization_barrier((weight, left_sum))
    left_part = lax.ppermute(left_sum, PLANE, back)
    piece = latent * amino // row_count
    left_pieces = left_part.reshape(share, row_count, piece).transpose(1, 0, 2)
    right_pieces = grads[..., latent * amino :].reshape(depth_count, share, row_count // depth_count, piece)
    right_pieces = right_pieces.transpose(0, 2, 1, 3).reshape(row_count, share, piece)
    pieces = jnp.concatenate([left_pieces, right_pieces], axis=-1)
    turned = lax.dynamic_slice_in_dim(jnp.concatenate([pieces, pieces]), lax.axis_index("row"), row_count, 0)
    reduced = turned[0].astype(F32)
    for k in range(1, row_count):
        reduced = reduced + shifted(turned[k], "row", k).astype(F32)
    reduced = reduced.astype(BF)
    grads = exchange(copies(reduced, row_count), "row")
    left_full = grads[..., :piece].reshape(row_count, share, latent // row_count, amino)
    left_full = left_full.transpose(1, 0, 2, 3).reshape(share, latent, amino)
    right_full = grads[..., piece:].reshape(row_count, share, amino // row_count, latent)
    right_full = right_full.transpose(1, 0, 2, 3).reshape(share, amino, latent)
    alignment_adjoint = align_of(alignment_matrix, left_full, right_full, weights_t)

    bias = jnp.sum(adjoint_incoming.astype(F32), axis=(0, 1)).astype(BF)
    rows = kron // plane_count
    bias_rows = jnp.broadcast_to(bias[None, None], (plane_count, 8, width))
    sent = jnp.concatenate([weight.reshape(plane_count, rows, width), bias_rows], axis=1)
    received = exchange(sent, PLANE)
    mine = jnp.sum(received.astype(F32), axis=0)
    total = ((mine + shifted(mine, "depth", 2)) + (shifted(mine, "depth", 1) + shifted(mine, "depth", 3))) / crop_length
    weight_gradient = exchange(copies(total[:rows].astype(BF), plane_count), PLANE)
    weight_gradient = weight_gradient.reshape(kron, width).astype(F32)
    return contact_delta, alignment_adjoint, weight_gradient, total[rows]


def solution(mesh):
    in_specs = (P("depth", "col", None), P(), P(), P(), P("row", ("col", "depth"), None))
    out_specs = (P("row", ("col", "depth"), None), P("depth", "col", None), P(), P())
    return jax.shard_map(step, mesh=mesh, in_specs=in_specs, out_specs=out_specs, check_vma=False)
```

time: 474 us -> 157 us (0.33)
  waiting for transfers between devices: 243 us -> 29 us
  blocking collectives: 79.8 us -> 0 us
  starting transfers between devices: 18.3 us -> 73.4 us
  local copies, waits for them, and re-layouts: 57 us -> 12 us
  matrix products: 36.2 us -> 3.4 us
  Pallas kernels: 0 us -> 32.5 us
  other arithmetic: 21.6 us -> 5.17 us
  between operations: 15.8 us -> 0.93 us
    psum x1 -> x0, waiting for transfers between devices: 205 us -> none  [in_one(): running = lax.psum(vector, axis)]
    psum x1 -> x0, blocking collectives: 66 us -> none  [body(): left_summed = lax.psum(left_back, 'col')]
    dot_general x8 -> x1, matrix products: 36.2 us -> 3.4 us  [step(): lax.dot_general(left, grad_outer, (((1,), (0,)), ((), ())), preferred_ele...]
    pallas_call x0 -> x4, Pallas kernels: none -> 32.5 us  [the longest x1 10.2 us: outer_of(): pl.pallas_call(lambda *refs: outer_kernel(scale, *refs), grid=(left.shape...]
    ppermute x0 -> x12, starting transfers between devices: none -> 31.3 us  [the longest x10 22.8 us: shifted(): return lax.ppermute(value, axis, [(q, (q + by) % n) for q in range(n)])]
    convert_element_type x3 -> x0, local copies, waits for them, and re-layouts: 29.6 us -> none  [the longest x1 20.1 us: body(): outer_mean = (summed / seq_count).astype(jnp.bfloat16)]
    all_to_all x4 -> x6, starting transfers between devices: 17.9 us -> 42.1 us  [exchange(): return lax.all_to_all(pieces, axis, split_axis=0, concat_axis=0, tiled=True)]
    ppermute x0 -> x12, waiting for transfers between devices: none -> 17.5 us  [the longest x1 9.71 us: step(): left_part = lax.ppermute(left_sum, PLANE, back)]
  transfers between devices with their start and end apart: 7 -> 18, of which waited for: 3 -> 10; matrix products, arithmetic and copies ran while one was open for 15% -> 6% of each run, Pallas kernels for 0% -> 18%
where the time goes in v1:
time: 157 us; the launch traced here: 156 us
  starting transfers between devices  73.4 us (47%)
  Pallas kernels  32.5 us (21%)
  waiting for transfers between devices  29 us (18%)
  local copies, waits for them, and re-layouts  12 us (8%)
  other arithmetic  5.17 us (3%)
  matrix products  3.4 us (2%)
    all_to_all x6, starting transfers between devices, exchange(): return lax.all_to_all(pieces, axis, split_axis=0, concat_axis=0, tiled=True)  42.1 us
    ppermute x10, starting transfers between devices, shifted(): return lax.ppermute(value, axis, [(q, (q + by) % n) for q in range(n)])  22.8 us
    all_to_all x6, waiting for transfers between devices, exchange(): return lax.all_to_all(pieces, axis, split_axis=0, concat_axis=0, tiled=True)  11.5 us
    pallas_call x1, Pallas kernels, outer_of(): pl.pallas_call(lambda *refs: outer_kernel(scale, *refs), grid=(left.shape...  10.2 us
    pallas_call x1, Pallas kernels, grad_outer_of(): pl.pallas_call(lambda *refs: grad_outer_kernel(scale, *refs), grid=(group...  9.75 us
    ppermute x1, waiting for transfers between devices, step(): left_part = lax.ppermute(left_sum, PLANE, back)  9.71 us
    ppermute x10, waiting for transfers between devices, shifted(): return lax.ppermute(value, axis, [(q, (q + by) % n) for q in range(n)])  7.78 us
    pallas_call x1, Pallas kernels, align_of(): pl.pallas_call(align_kernel, grid=(share // 8,), in_specs=[pl.BlockSpec((...  7.47 us
  transfers between devices with their start and end apart: 18, of which 10 were waited for; matrix products, arithmetic and copies ran while one was open for 6% of the time, Pallas kernels for 18%

profile of v1, /device:TPU:1, one launch (start us, length us, event | category | flops | bytes accessed | tf_op | source)
XLA Modules:
  0.0 156.3 jit_solution(5686619346819280324)
XLA Ops:
  0.6 5.1 %panels.1 = (bf16[32,32,96]{2,1,0:T(8,128)(2,1)}, bf16[32,96,32]{2,1,0:T(8,128)(2,1)}) custom-call(bf16[32,96,256]{2,1,0:T(8,128)(2,1)} %align_ref.3, bf16[64,256]{1,0:T(8,128)(2,1)} %bitcast.80), custom_call_target="tpu_custom_call" | custom-call | tf_op jit(solution)/shard_map/panels/pallas_call | solution.py:49
  5.7 1.3 reshape.59
  7.0 4.9 %collective-permute-start = (bf16[32,3072]{1,0:T(8,128)(2,1)S(1)}, bf16[32,3072]{1,0:T(8,128)(2,1)S(1)}, u32[]{:S(2)}, u32[]{:S(2)}) collective-permute-start(bf16[32,3072]{1,0:T(8,128)(2,1)S(1)} %reshape.59), channel_id=1, source_target_pairs={{0,0},{32,4},{64,8},{96,12},{128,16},{160,20},{192,24},{224,28},{4... | collective-permute-start | bytes 589832 | tf_op jit(solution)/shard_map/ppermute | solution.py:231
  11.9 1.6 %reshape.57 = bf16[32,4,768]{2,1,0:T(4,128)(2,1)S(1)} reshape(bf16[32,96,32]{2,1,0:T(8,128)(2,1)} %get-tuple-element.15) | data formatting | bytes 393216 | tf_op jit(solution)/shard_map/reshape | solution.py:232
  13.6 0.7 copy.96
  14.3 4.2 %all-to-all-start = ((bf16[4,32,768]{2,1,0:T(8,128)(2,1)}), bf16[4,32,768]{2,1,0:T(8,128)(2,1)S(1)}, u32[]{:S(2)}, u32[]{:S(2)}) async-start(bf16[4,32,768]{2,1,0:T(8,128)(2,1)} %copy.96), calls=%async_computation | async-start | bytes 393216 | tf_op jit(solution)/shard_map/all_to_all | solution.py:209
  18.5 0.9 copy.120
  19.4 4.3 %all-to-all-done = bf16[4,32,768]{2,1,0:T(8,128)(2,1)S(1)} async-done(((bf16[4,32,768]{2,1,0:T(8,128)(2,1)}), bf16[4,32,768]{2,1,0:T(8,128)(2,1)S(1)}, u32[]{:S(2)}, u32[]{:S(2)}) %all-to-all-start) | async-done | bytes 196640 | tf_op jit(solution)/shard_map/all_to_all | solution.py:209
  23.6 1.0 broadcast_in_dim.8
  24.6 3.5 %all-to-all-start.1 = ((bf16[4,32,3072]{2,1,0:T(8,128)(2,1)}), bf16[4,32,3072]{2,1,0:T(8,128)(2,1)S(1)}, u32[]{:S(2)}, u32[]{:S(2)}) async-start(bf16[4,32,3072]{2,1,0:T(8,128)(2,1)} %broadcast_in_dim.8), calls=%async_computation.1 | async-start | bytes 1572864 | tf_op jit(solution)/shard_map/all_to_all | solution.py:209
  28.1 9.7 %grad_outer.1 = (bf16[3072,768]{1,0:T(8,128)(2,1)}, bf16[128,3072]{1,0:T(8,128)(2,1)}) custom-call(bf16[24,96,128]{2,1,0:T(8,128)(2,1)} %bitcast.67, bf16[1024,128]{1,0:T(8,128)(2,1)} %refs_1_.1, bf16[128,768]{1,0:T(8,128)(2,1)} %bitcast.71), custom_call_target="tpu_custom_call" | custom-call | tf_op jit(solution)/shard_map/grad_outer/pallas_call | solution.py:126
  37.9 2.5 %all-to-all-done.1 = bf16[4,32,3072]{2,1,0:T(8,128)(2,1)S(1)} async-done(((bf16[4,32,3072]{2,1,0:T(8,128)(2,1)}), bf16[4,32,3072]{2,1,0:T(8,128)(2,1)S(1)}, u32[]{:S(2)}, u32[]{:S(2)}) %all-to-all-start.1) | async-done | bytes 786464 | tf_op jit(solution)/shard_map/all_to_all | solution.py:209
  40.3 3.4 %convolution_convert_fusion = bf16[128,768]{1,0:T(8,128)(2,1)S(1)} fusion(bf16[128,3072]{1,0:T(8,128)(2,1)S(1)} %bitcast.65, bf16[3072,768]{1,0:T(8,128)(2,1)} %get-tuple-element.23), kind=kOutput, calls=%fused_computation | convolution fusion | flops 604078080 | bytes 5701632 | tf_op jit(solution)/shard_map/dot_general | solution.py:239
  43.8 1.0 pad_maximum_fusion
  44.8 3.5 %all-to-all-start.2 = ((bf16[4,32,3840]{2,1,0:T(8,128)(2,1)}), bf16[4,32,3840]{2,1,0:T(8,128)(2,1)S(1)}, u32[]{:S(2)}, u32[]{:S(2)}) async-start(bf16[4,32,3840]{2,1,0:T(8,128)(2,1)} %bitcast.7), calls=%async_computation.2 | async-start | bytes 1966080 | tf_op jit(solution)/shard_map/all_to_all | solution.py:209
  48.3 0.3 reduce_sum.34
  48.6 10.2 %outer.1 = (bf16[24,96,128]{2,1,0:T(8,128)(2,1)}, bf16[1024,128]{1,0:T(8,128)(2,1)}) custom-call(bf16[128,3072]{1,0:T(8,128)(2,1)} %bitcast.66, bf16[128,768]{1,0:T(8,128)(2,1)} %bitcast.72, bf16[24,96,128]{2,1,0:T(8,128)(2,1)} %bitcast.68, bf16[1024,128]{1,0:T(8,128)(2,1)} %refs_1_.1, f32[1,128]{1,0:T(1,128)} %bitcast.89), custom_call_target="tpu_custom_call" | custom-call | tf_op jit(solution)/shard_map/outer/pallas_call | solution.py:177
  58.8 3.6 %all-to-all-done.2 = bf16[4,32,3840]{2,1,0:T(8,128)(2,1)S(1)} async-done(((bf16[4,32,3840]{2,1,0:T(8,128)(2,1)}), bf16[4,32,3840]{2,1,0:T(8,128)(2,1)S(1)}, u32[]{:S(2)}, u32[]{:S(2)}) %all-to-all-start.2) | async-done | bytes 983072 | tf_op jit(solution)/shard_map/all_to_all | solution.py:209
  62.5 1.7 %pad_maximum_fusion.1 = bf16[64,24,128]{2,1,0:T(8,128)(2,1)} fusion(bf16[64,8,128]{2,1,0:T(8,128)(2,1)S(1)} %broadcast_in_dim.10, bf16[64,16,128]{2,1,0:T(8,128)(2,1)} %bitcast.78), kind=kLoop, calls=%fused_computation.12 | loop fusion | flops 786432 | bytes 786432 | tf_op jit(solution)/shard_map/concatenate | solution.py:268
  64.2 13.2 %all-to-all-start.4 = ((bf16[64,24,128]{2,1,0:T(8,128)(2,1)}), bf16[64,24,128]{2,1,0:T(8,128)(2,1)S(1)}, u32[]{:S(2)}, u32[]{:S(2)}) async-start(bf16[64,24,128]{2,1,0:T(8,128)(2,1)} %pad_maximum_fusion.1), calls=%async_computation.4 | async-start | bytes 786432 | tf_op jit(solution)/shard_map/all_to_all | solution.py:209
  77.5 3.5 %collective-permute-start.1 = (bf16[32,3072]{1,0:T(8,128)(2,1)S(1)}, bf16[32,3072]{1,0:T(8,128)(2,1)S(1)}, u32[]{:S(2)}, u32[]{:S(2)}) collective-permute-start(bf16[32,3072]{1,0:T(8,128)(2,1)S(1)} %slice_reduce_fusion), channel_id=1, source_target_pairs={{0,0},{4,32},{8,64},{12,96},{16,128},{20,160},{24,192},{28,224},{3... | collective-permute-start | bytes 589832 | tf_op jit(solution)/shard_map/ppermute | solution.py:247
  81.2 9.7 %collective-permute-done.1 = bf16[32,3072]{1,0:T(8,128)(2,1)S(1)} collective-permute-done((bf16[32,3072]{1,0:T(8,128)(2,1)S(1)}, bf16[32,3072]{1,0:T(8,128)(2,1)S(1)}, u32[]{:S(2)}, u32[]{:S(2)}) %collective-permute-start.1) | collective-permute-done | bytes 196640 | tf_op jit(solution)/shard_map/ppermute | solution.py:247
  90.9 0.4 fusion.1
  91.3 0.6 fusion.12
  92.0 10.6 %collective-permute-start.3 = (bf16[32,768]{1,0:T(8,128)(2,1)S(1)}, bf16[32,768]{1,0:T(8,128)(2,1)S(1)}, u32[]{:S(2)}, u32[]{:S(2)}) collective-permute-start(bf16[32,768]{1,0:T(8,128)(2,1)S(1)} %bitcast.83), channel_id=1, source_target_pairs={{0,64},{32,96},{64,128},{96,160},{128,192},{160,224},{192,0},{224,... | collective-permute-start | bytes 147464 | tf_op jit(solution)/shard_map/ppermute | solution.py:196
  102.6 4.8 %collective-permute-start.4 = (bf16[32,768]{1,0:T(8,128)(2,1)S(1)}, bf16[32,768]{1,0:T(8,128)(2,1)S(1)}, u32[]{:S(2)}, u32[]{:S(2)}) collective-permute-start(bf16[32,768]{1,0:T(8,128)(2,1)S(1)} %bitcast.82), channel_id=1, source_target_pairs={{0,96},{32,128},{64,160},{96,192},{128,224},{160,0},{192,32},{224,... | collective-permute-start | bytes 147464 | tf_op jit(solution)/shard_map/ppermute | solution.py:196
  107.5 4.1 %collective-permute-start.6 = (bf16[32,768]{1,0:T(8,128)(2,1)S(1)}, bf16[32,768]{1,0:T(8,128)(2,1)S(1)}, u32[]{:S(2)}, u32[]{:S(2)}) collective-permute-start(bf16[32,768]{1,0:T(8,128)(2,1)S(1)} %bitcast.86), channel_id=1, source_target_pairs={{0,160},{32,192},{64,224},{96,0},{128,32},{160,64},{192,96},{224,1... | collective-permute-start | bytes 147464 | tf_op jit(solution)/shard_map/ppermute | solution.py:196
  111.8 0.3 collective-permute-start.8
  112.1 0.4 collective-permute-done.5
  112.5 0.3 collective-permute-done.6
  112.8 2.9 %collective-permute-done.7 = bf16[32,768]{1,0:T(8,128)(2,1)S(1)} collective-permute-done((bf16[32,768]{1,0:T(8,128)(2,1)S(1)}, bf16[32,768]{1,0:T(8,128)(2,1)S(1)}, u32[]{:S(2)}, u32[]{:S(2)}) %collective-permute-start.7) | collective-permute-done | bytes 49184 | tf_op jit(solution)/shard_map/ppermute | solution.py:196
  115.8 0.8 broadcast_in_dim.9
  116.6 3.5 %all-to-all-start.3 = ((bf16[8,32,768]{2,1,0:T(8,128)(2,1)}), bf16[8,32,768]{2,1,0:T(8,128)(2,1)S(1)}, u32[]{:S(2)}, u32[]{:S(2)}) async-start(bf16[8,32,768]{2,1,0:T(8,128)(2,1)} %broadcast_in_dim.9), calls=%async_computation.3 | async-start | bytes 786432 | tf_op jit(solution)/shard_map/all_to_all | solution.py:209
  120.1 0.4 collective-permute-start.10
  120.5 2.4 %collective-permute-start.11 = (f32[24,128]{1,0:T(8,128)S(1)}, f32[24,128]{1,0:T(8,128)S(1)}, u32[]{:S(2)}, u32[]{:S(2)}) collective-permute-start(f32[24,128]{1,0:T(8,128)S(1)} %convert_reduce_fusion), channel_id=1, source_target_pairs={{0,3},{1,0},{2,1},{3,2},{4,7},{5,4},{6,5},{7,6},{8,11},{9,8},{10,9... | collective-permute-start | bytes 36872 | tf_op jit(solution)/shard_map/ppermute | solution.py:196
  122.9 1.1 collective-permute-done.10
  124.0 3.0 %collective-permute-done.9 = f32[24,128]{1,0:T(8,128)S(1)} collective-permute-done((f32[24,128]{1,0:T(8,128)S(1)}, f32[24,128]{1,0:T(8,128)S(1)}, u32[]{:S(2)}, u32[]{:S(2)}) %collective-permute-start.9) | collective-permute-done | bytes 12320 | tf_op jit(solution)/shard_map/ppermute | solution.py:196
  127.1 0.7 broadcast_in_dim.11
  127.8 14.2 %all-to-all-start.5 = ((bf16[64,16,128]{2,1,0:T(8,128)(2,1)}), bf16[64,16,128]{2,1,0:T(8,128)(2,1)S(1)}, u32[]{:S(2)}, u32[]{:S(2)}) async-start(bf16[64,16,128]{2,1,0:T(8,128)(2,1)} %broadcast_in_dim.11), calls=%async_computation.5 | async-start | bytes 524288 | tf_op jit(solution)/shard_map/all_to_all | solution.py:209
  142.0 1.0 copy.101
  143.1 0.5 slice_bitcast_fusion
  143.6 0.8 reshape.67
  144.4 0.2 copy.99
  144.6 1.2 copy.100.right_ref
  146.0 0.8 copy.98
  146.8 7.5 %align.1 = f32[32,96,256]{2,1,0:T(8,128)} custom-call(bf16[32,96,256]{2,1,0:T(8,128)(2,1)} %align_ref.3, bf16[32,32,96]{2,1,0:T(8,128)(2,1)} %bitcast.73, bf16[32,96,32]{2,1,0:T(8,128)(2,1)} %copy.100.right_ref, bf16[64,256]{1,0:T(8,128)(2,1)} %bitcast.81), custom_call_target="tpu_custom_call" | custom-call | tf_op jit(solution)/shard_map/align/pallas_call | solution.py:81
  154.3 1.2 all-to-all-done.5
  155.4 0.8 bitcast_convert_fusion
  (41 shorter events, 1.0 us)
Async XLA Ops:
  0.6 17.8 %copy-start.1 = (bf16[96,24,128]{2,1,0:T(8,128)(2,1)S(1)}, bf16[96,24,128]{2,1,0:T(8,128)(2,1)}, u32[]{:S(2)}) copy-start(bf16[96,24,128]{2,1,0:T(8,128)(2,1)} %param.9) | copy-start | bytes 1769476
  7.0 16.7 %collective-permute-start = (bf16[32,3072]{1,0:T(8,128)(2,1)S(1)}, bf16[32,3072]{1,0:T(8,128)(2,1)S(1)}, u32[]{:S(2)}, u32[]{:S(2)}) collective-permute-start(bf16[32,3072]{1,0:T(8,128)(2,1)S(1)} %reshape.59), channel_id=1, source_target_pairs={{0,0},{32,4},{64,8},{96,12},{128,16},{160,20},{192,24},{224,28},{4... | collective-permute-start | bytes 589832 | tf_op jit(solution)/shard_map/ppermute | solution.py:231
  14.3 9.4 %all-to-all-start = ((bf16[4,32,768]{2,1,0:T(8,128)(2,1)}), bf16[4,32,768]{2,1,0:T(8,128)(2,1)S(1)}, u32[]{:S(2)}, u32[]{:S(2)}) async-start(bf16[4,32,768]{2,1,0:T(8,128)(2,1)} %copy.96), calls=%async_computation | async-start | bytes 393216 | tf_op jit(solution)/shard_map/all_to_all | solution.py:209
  23.6 4.5 %copy-start.2 = (bf16[4,32,768]{2,1,0:T(8,128)(2,1)}, bf16[4,32,768]{2,1,0:T(8,128)(2,1)S(1)}, u32[]{:S(2)}) copy-start(bf16[4,32,768]{2,1,0:T(8,128)(2,1)S(1)} %all-to-all-done) | copy-start | bytes 589828
  24.6 15.7 %all-to-all-start.1 = ((bf16[4,32,3072]{2,1,0:T(8,128)(2,1)}), bf16[4,32,3072]{2,1,0:T(8,128)(2,1)S(1)}, u32[]{:S(2)}, u32[]{:S(2)}) async-start(bf16[4,32,3072]{2,1,0:T(8,128)(2,1)} %broadcast_in_dim.8), calls=%async_computation.1 | async-start | bytes 1572864 | tf_op jit(solution)/shard_map/all_to_all | solution.py:209
  37.9 5.9 %copy-start.3 = (bf16[128,3072]{1,0:T(8,128)(2,1)S(1)}, bf16[128,3072]{1,0:T(8,128)(2,1)}, u32[]{:S(2)}) copy-start(bf16[128,3072]{1,0:T(8,128)(2,1)} %get-tuple-element.22) | copy-start | bytes 2359300
  40.3 4.4 %copy-start = (bf16[4,32,3072]{2,1,0:T(8,128)(2,1)}, bf16[4,32,3072]{2,1,0:T(8,128)(2,1)S(1)}, u32[]{:S(2)}) copy-start(bf16[4,32,3072]{2,1,0:T(8,128)(2,1)S(1)} %all-to-all-done.1) | copy-start | bytes 2359300
  44.8 17.6 %all-to-all-start.2 = ((bf16[4,32,3840]{2,1,0:T(8,128)(2,1)}), bf16[4,32,3840]{2,1,0:T(8,128)(2,1)S(1)}, u32[]{:S(2)}, u32[]{:S(2)}) async-start(bf16[4,32,3840]{2,1,0:T(8,128)(2,1)} %bitcast.7), calls=%async_computation.2 | async-start | bytes 1966080 | tf_op jit(solution)/shard_map/all_to_all | solution.py:209
  64.2 51.6 %all-to-all-start.4 = ((bf16[64,24,128]{2,1,0:T(8,128)(2,1)}), bf16[64,24,128]{2,1,0:T(8,128)(2,1)S(1)}, u32[]{:S(2)}, u32[]{:S(2)}) async-start(bf16[64,24,128]{2,1,0:T(8,128)(2,1)} %pad_maximum_fusion.1), calls=%async_computation.4 | async-start | bytes 786432 | tf_op jit(solution)/shard_map/all_to_all | solution.py:209
  77.5 13.4 %collective-permute-start.1 = (bf16[32,3072]{1,0:T(8,128)(2,1)S(1)}, bf16[32,3072]{1,0:T(8,128)(2,1)S(1)}, u32[]{:S(2)}, u32[]{:S(2)}) collective-permute-start(bf16[32,3072]{1,0:T(8,128)(2,1)S(1)} %slice_reduce_fusion), channel_id=1, source_target_pairs={{0,0},{4,32},{8,64},{12,96},{16,128},{20,160},{24,192},{28,224},{3... | collective-permute-start | bytes 589832 | tf_op jit(solution)/shard_map/ppermute | solution.py:247
  90.9 51.1 %copy-start.4 = (bf16[24,96,128]{2,1,0:T(8,128)(2,1)S(1)}, bf16[24,96,128]{2,1,0:T(8,128)(2,1)}, u32[]{:S(2)}) copy-start(bf16[24,96,128]{2,1,0:T(8,128)(2,1)} %get-tuple-element.20) | copy-start | bytes 1769476
  91.9 19.7 %collective-permute-start.2 = (bf16[32,768]{1,0:T(8,128)(2,1)S(1)}, bf16[32,768]{1,0:T(8,128)(2,1)S(1)}, u32[]{:S(2)}, u32[]{:S(2)}) collective-permute-start(bf16[32,768]{1,0:T(8,128)(2,1)S(1)} %bitcast.85), channel_id=1, source_target_pairs={{0,32},{32,64},{64,96},{96,128},{128,160},{160,192},{192,224},{224... | collective-permute-start | bytes 147464 | tf_op jit(solution)/shard_map/ppermute | solution.py:196
  92.0 19.7 %collective-permute-start.3 = (bf16[32,768]{1,0:T(8,128)(2,1)S(1)}, bf16[32,768]{1,0:T(8,128)(2,1)S(1)}, u32[]{:S(2)}, u32[]{:S(2)}) collective-permute-start(bf16[32,768]{1,0:T(8,128)(2,1)S(1)} %bitcast.83), channel_id=1, source_target_pairs={{0,64},{32,96},{64,128},{96,160},{128,192},{160,224},{192,0},{224,... | collective-permute-start | bytes 147464 | tf_op jit(solution)/shard_map/ppermute | solution.py:196
  102.6 9.5 %collective-permute-start.4 = (bf16[32,768]{1,0:T(8,128)(2,1)S(1)}, bf16[32,768]{1,0:T(8,128)(2,1)S(1)}, u32[]{:S(2)}, u32[]{:S(2)}) collective-permute-start(bf16[32,768]{1,0:T(8,128)(2,1)S(1)} %bitcast.82), channel_id=1, source_target_pairs={{0,96},{32,128},{64,160},{96,192},{128,224},{160,0},{192,32},{224,... | collective-permute-start | bytes 147464 | tf_op jit(solution)/shard_map/ppermute | solution.py:196
  107.4 5.1 %collective-permute-start.5 = (bf16[32,768]{1,0:T(8,128)(2,1)S(1)}, bf16[32,768]{1,0:T(8,128)(2,1)S(1)}, u32[]{:S(2)}, u32[]{:S(2)}) collective-permute-start(bf16[32,768]{1,0:T(8,128)(2,1)S(1)} %bitcast.84), channel_id=1, source_target_pairs={{0,128},{32,160},{64,192},{96,224},{128,0},{160,32},{192,64},{224,... | collective-permute-start | bytes 147464 | tf_op jit(solution)/shard_map/ppermute | solution.py:196
  107.5 5.3 %collective-permute-start.6 = (bf16[32,768]{1,0:T(8,128)(2,1)S(1)}, bf16[32,768]{1,0:T(8,128)(2,1)S(1)}, u32[]{:S(2)}, u32[]{:S(2)}) collective-permute-start(bf16[32,768]{1,0:T(8,128)(2,1)S(1)} %bitcast.86), channel_id=1, source_target_pairs={{0,160},{32,192},{64,224},{96,0},{128,32},{160,64},{192,96},{224,1... | collective-permute-start | bytes 147464 | tf_op jit(solution)/shard_map/ppermute | solution.py:196
  111.7 4.1 %collective-permute-start.7 = (bf16[32,768]{1,0:T(8,128)(2,1)S(1)}, bf16[32,768]{1,0:T(8,128)(2,1)S(1)}, u32[]{:S(2)}, u32[]{:S(2)}) collective-permute-start(bf16[32,768]{1,0:T(8,128)(2,1)S(1)} %bitcast.88), channel_id=1, source_target_pairs={{0,192},{32,224},{64,0},{96,32},{128,64},{160,96},{192,128},{224,1... | collective-permute-start | bytes 147464 | tf_op jit(solution)/shard_map/ppermute | solution.py:196
  111.8 4.0 %collective-permute-start.8 = (bf16[32,768]{1,0:T(8,128)(2,1)S(1)}, bf16[32,768]{1,0:T(8,128)(2,1)S(1)}, u32[]{:S(2)}, u32[]{:S(2)}) collective-permute-start(bf16[32,768]{1,0:T(8,128)(2,1)S(1)} %bitcast.87), channel_id=1, source_target_pairs={{0,224},{32,0},{64,32},{96,64},{128,96},{160,128},{192,160},{224,1... | collective-permute-start | bytes 147464 | tf_op jit(solution)/shard_map/ppermute | solution.py:196
  116.6 10.4 %all-to-all-start.3 = ((bf16[8,32,768]{2,1,0:T(8,128)(2,1)}), bf16[8,32,768]{2,1,0:T(8,128)(2,1)S(1)}, u32[]{:S(2)}, u32[]{:S(2)}) async-start(bf16[8,32,768]{2,1,0:T(8,128)(2,1)} %broadcast_in_dim.9), calls=%async_computation.3 | async-start | bytes 786432 | tf_op jit(solution)/shard_map/all_to_all | solution.py:209
  120.1 3.8 %collective-permute-start.10 = (f32[24,128]{1,0:T(8,128)S(1)}, f32[24,128]{1,0:T(8,128)S(1)}, u32[]{:S(2)}, u32[]{:S(2)}) collective-permute-start(f32[24,128]{1,0:T(8,128)S(1)} %convert_reduce_fusion), channel_id=1, source_target_pairs={{0,1},{1,2},{2,3},{3,0},{4,5},{5,6},{6,7},{7,4},{8,9},{9,10},{10,1... | collective-permute-start | bytes 36872 | tf_op jit(solution)/shard_map/ppermute | solution.py:196
  120.5 3.5 %collective-permute-start.11 = (f32[24,128]{1,0:T(8,128)S(1)}, f32[24,128]{1,0:T(8,128)S(1)}, u32[]{:S(2)}, u32[]{:S(2)}) collective-permute-start(f32[24,128]{1,0:T(8,128)S(1)} %convert_reduce_fusion), channel_id=1, source_target_pairs={{0,3},{1,0},{2,1},{3,2},{4,7},{5,4},{6,5},{7,6},{8,11},{9,8},{10,9... | collective-permute-start | bytes 36872 | tf_op jit(solution)/shard_map/ppermute | solution.py:196
  122.9 4.1 %collective-permute-start.9 = (f32[24,128]{1,0:T(8,128)S(1)}, f32[24,128]{1,0:T(8,128)S(1)}, u32[]{:S(2)}, u32[]{:S(2)}) collective-permute-start(f32[24,128]{1,0:T(8,128)S(1)} %convert_reduce_fusion), channel_id=1, source_target_pairs={{0,2},{1,3},{2,0},{3,1},{4,6},{5,7},{6,4},{7,5},{8,10},{9,11},{10,... | collective-permute-start | bytes 36872 | tf_op jit(solution)/shard_map/ppermute | solution.py:196
  127.8 27.6 %all-to-all-start.5 = ((bf16[64,16,128]{2,1,0:T(8,128)(2,1)}), bf16[64,16,128]{2,1,0:T(8,128)(2,1)S(1)}, u32[]{:S(2)}, u32[]{:S(2)}) async-start(bf16[64,16,128]{2,1,0:T(8,128)(2,1)} %broadcast_in_dim.11), calls=%async_computation.5 | async-start | bytes 524288 | tf_op jit(solution)/shard_map/all_to_all | solution.py:209

commit v2 on v1

--- a/solution.py
+++ b/solution.py
@@ -112,32 +112,35 @@
     final = final_ref[...]
     for four in range(quarter // 4):
         adj = adj_ref[four * 4 : (four + 1) * 4].reshape(4 * block_i, width)
-        g = lax.dot_general(adj, final, NT, preferred_element_type=F32) * scale
-        tiles = [g[j * block_i : (j + 1) * block_i] for j in range(4)]
-        for c, tile in enumerate(swap_blocks(tiles)):
-            outer_ref[c * block_i : (c + 1) * block_i, four * 128 : (four + 1) * 128] = tile.astype(BF)
-    left_ref[...] = lax.dot_general(right_ref[...], outer_ref[...], NT, preferred_element_type=F32).astype(BF)
+        g = lax.dot_general(adj, final, NT, preferred_element_type=F32).astype(BF)
+        for part in range(final.shape[0] // 128):
+            tiles = [g[j * block_i : (j + 1) * block_i, part * 128 : (part + 1) * 128] for j in range(4)]
+            for c, tile in enumerate(swap_blocks(tiles)):
+                at = (part * 4 + c) * block_i
+                outer_ref[at : at + block_i, four * 128 : (four + 1) * 128] = tile
+    left = lax.dot_general(right_ref[...], outer_ref[...], NT, preferred_element_type=F32)
+    left_ref[...] = (left * scale).astype(BF)
 
 
 def grad_outer_of(adj, final, right, scale):
     _, block_i, width = adj.shape
     seqs, lanes = right.shape
-    groups = final.shape[0] // 128
+    groups = final.shape[0] // 256
     return pl.pallas_call(
         lambda *refs: grad_outer_kernel(scale, *refs),
         grid=(groups,),
         in_specs=[
             pl.BlockSpec(adj.shape, lambda g: (0, 0, 0)),
-            pl.BlockSpec((128, width), lambda g: (g, 0)),
+            pl.BlockSpec((256, width), lambda g: (g, 0)),
             pl.BlockSpec(right.shape, lambda g: (0, 0)),
         ],
         out_specs=[
-            pl.BlockSpec((4 * block_i, lanes), lambda g: (g, 0)),
-            pl.BlockSpec((seqs, 4 * block_i), lambda g: (0, g)),
+            pl.BlockSpec((8 * block_i, lanes), lambda g: (g, 0)),
+            pl.BlockSpec((seqs, 8 * block_i), lambda g: (0, g)),
         ],
         out_shape=[
-            jax.ShapeDtypeStruct((groups * 4 * block_i, lanes), BF),
-            jax.ShapeDtypeStruct((seqs, groups * 4 * block_i), BF),
+            jax.ShapeDtypeStruct((groups * 8 * block_i, lanes), BF),
+            jax.ShapeDtypeStruct((seqs, groups * 8 * block_i), BF),
         ],
         name="grad_outer",
     )(adj, final, right)
@@ -149,12 +152,12 @@
     column = pl.ds(pl.multiple_of(step * 128, 128), 128)
     left = left_ref[...]
     for pair in range(quarter // 8):
-        o = lax.dot_general(left, right_ref[:, pair * 256 : (pair + 1) * 256], TN, preferred_element_type=F32) * scale
+        o = lax.dot_general(left, right_ref[:, pair * 256 : (pair + 1) * 256], TN, preferred_element_type=F32).astype(BF)
         for part in range(2):
             tiles = [o[c * block_i : (c + 1) * block_i, part * 128 : (part + 1) * 128] for c in range(4)]
             for j, tile in enumerate(swap_blocks(tiles)):
                 at = ((pair * 2 + part) * 4 + j) * block_i
-                outer_ref[at : at + block_i, column] = tile.astype(BF)
+                outer_ref[at : at + block_i, column] = tile
 
     @pl.when(step == pl.num_programs(0) - 1)
     def _():
@@ -163,15 +166,21 @@
             rows = slice(pair * 8 * block_i, (pair + 1) * 8 * block_i)
             outer = outer_ref[rows, :]
             adj = adj_ref[pair * 8 : (pair + 1) * 8].reshape(8 * block_i, width)
-            pairs = jnp.dot(outer, final_ref[...], preferred_element_type=F32) + offset_ref[...]
+            pairs = jnp.dot(outer, final_ref[...], preferred_element_type=F32) * scale + offset_ref[...]
             pair_ref[pair * 8 : (pair + 1) * 8] = pairs.astype(BF).reshape(8, block_i, width)
             part = lax.dot_general(adj, outer, TN, preferred_element_type=F32)
             weight = part if weight is None else weight + part
-        weight_ref[...] = weight.T.astype(BF)
-
-
-def outer_of(left, right, adj, final, offset, scale):
+        weight = (weight * scale).T.astype(BF)
+        bias = jnp.sum(adj_ref[...].astype(F32).reshape(quarter * block_i, width), axis=0, keepdims=True)
+        bias = jnp.broadcast_to(bias.astype(BF), (8, width))
+        pieces, rows = weight_ref.shape[0], weight_ref.shape[1] - 8
+        for p in range(pieces):
+            weight_ref[p] = jnp.concatenate([weight[p * rows : (p + 1) * rows], bias])
+
+
+def outer_of(left, right, adj, final, offset, scale, pieces):
     quarter, block_i, width = adj.shape
+    weight = (pieces, final.shape[0] // pieces + 8, width)
     seqs = left.shape[0]
     whole = lambda shape: pl.BlockSpec(shape, lambda g: (0,) * len(shape))
     return pl.pallas_call(
@@ -184,8 +193,8 @@
             whole(final.shape),
             whole((1, width)),
         ],
-        out_specs=[whole(adj.shape), whole(final.shape)],
-        out_shape=[jax.ShapeDtypeStruct(adj.shape, BF), jax.ShapeDtypeStruct(final.shape, BF)],
+        out_specs=[whole(adj.shape), whole(weight)],
+        out_shape=[jax.ShapeDtypeStruct(adj.shape, BF), jax.ShapeDtypeStruct(weight, BF)],
         scratch_shapes=[pltpu.VMEM((quarter * block_i, final.shape[0]), BF)],
         name="outer",
     )(left, right, adj, final, offset.reshape(1, width))
@@ -200,7 +209,7 @@
     pairs = []
     for row in range(8):
         for col in range(8):
-            source_row = ((col // 2 + row // 2) % 4) * 2 + col % 2
+            source_row = ((row + 2 - col // 2 - row % 2) % 4) * 2 + col % 2
             pairs.append((source_row * 8 + row, row * 8 + col))
     return pairs
 
@@ -223,6 +232,7 @@
     _, quarter, width = adjoint_incoming.shape
     kron = final_matrix.shape[0]
     seq_count = share * depth_count
+    depth_idx = lax.axis_index("depth")
     there = crossings()
     back = [(b, a) for a, b in there]
 
@@ -230,16 +240,25 @@
     left_own, right_own = panels_of(alignment_matrix, weights_t)
     left_mine = lax.ppermute(left_own.reshape(share, latent * amino), PLANE, there)
     right_own = right_own.reshape(share, depth_count, quarter * latent).transpose(1, 0, 2)
-    right = exchange(right_own, "depth").reshape(seq_count, quarter * latent)
+    right = exchange(right_own, "depth")
+
+    def turned_back(chunks):
+        chunks = chunks.reshape(depth_count, share, -1)[::-1]
+        start = depth_count - 1 - depth_idx
+        return lax.dynamic_slice_in_dim(jnp.concatenate([chunks, chunks]), start, depth_count, 0)
+
+    right_turned = turned_back(right).reshape(seq_count, quarter * latent)
+    right = right.reshape(seq_count, quarter * latent)
 
     adj = jnp.transpose(adjoint_incoming, (1, 0, 2))
-    adj, right, left_mine = lax.optimization_barrier((adj, right, left_mine))
-    left = exchange(copies(left_mine, depth_count), "depth").reshape(seq_count, latent * amino)
+    adj, left_mine = lax.optimization_barrier((adj, left_mine))
+    left = jnp.concatenate([left_mine] + [shifted(left_mine, "depth", k) for k in range(1, depth_count)])
     grad_outer, grad_left = grad_outer_of(adj, final_matrix, right, 1.0 / seq_count)
-    grad_right = lax.dot_general(left, grad_outer, (((1,), (0,)), ((), ())), preferred_element_type=F32).astype(BF)
-    grads = jnp.concatenate([grad_left, grad_right], axis=-1).reshape(depth_count, share, -1)
-    grads = exchange(grads, "depth")
-    pair_t, weight = outer_of(left, right, adj, final_matrix, final_offset, 1.0 / seq_count)
+    grad_right = lax.dot_general(left, grad_outer, (((1,), (0,)), ((), ())), preferred_element_type=F32)
+    grad_right = (grad_right / seq_count).astype(BF)
+    grad_left = grad_left.reshape(depth_count, share, latent * amino)
+    grads = exchange(jnp.concatenate([grad_left, turned_back(grad_right)], axis=-1), "depth")
+    pair_t, weight = outer_of(left, right_turned, adj, final_matrix, final_offset, 1.0 / seq_count, plane_count)
     contact_delta = jnp.transpose(pair_t, (1, 0, 2))
 
     left_sum = jnp.sum(grads[..., : latent * amino].astype(F32), axis=0).astype(BF)
@@ -262,11 +281,8 @@
     right_full = right_full.transpose(1, 0, 2, 3).reshape(share, amino, latent)
     alignment_adjoint = align_of(alignment_matrix, left_full, right_full, weights_t)
 
-    bias = jnp.sum(adjoint_incoming.astype(F32), axis=(0, 1)).astype(BF)
     rows = kron // plane_count
-    bias_rows = jnp.broadcast_to(bias[None, None], (plane_count, 8, width))
-    sent = jnp.concatenate([weight.reshape(plane_count, rows, width), bias_rows], axis=1)
-    received = exchange(sent, PLANE)
+    received = exchange(weight, PLANE)
     mine = jnp.sum(received.astype(F32), axis=0)
     total = ((mine + shifted(mine, "depth", 2)) + (shifted(mine, "depth", 1) + shifted(mine, "depth", 3))) / crop_length
     weight_gradient = exchange(copies(total[:rows].astype(BF), plane_count), PLANE)

time: 157 us -> 147 us (0.936)
  waiting for transfers between devices: 29 us -> 23 us
  Pallas kernels: 32.5 us -> 30.4 us
    all_to_all x6 -> x5, starting transfers between devices: 42.1 us -> 34.9 us  [exchange(): return lax.all_to_all(pieces, axis, split_axis=0, concat_axis=0, tiled=True)]
    all_to_all x6 -> x5, waiting for transfers between devices: 11.5 us -> 4.55 us  [exchange(): return lax.all_to_all(pieces, axis, split_axis=0, concat_axis=0, tiled=True)]
    ppermute x1, waiting for transfers between devices: 9.71 us -> 13.2 us  [step(): left_part = lax.ppermute(left_sum, PLANE, back)]
    ppermute x1, starting transfers between devices: 4.93 us -> 7.92 us  [step(): lax.ppermute(left_own.reshape(share, latent * amino), PLANE, there)]
    ppermute x10 -> x13, waiting for transfers between devices: 7.78 us -> 5.25 us  [shifted(): return lax.ppermute(value, axis, [(q, (q + by) % n) for q in range(n)])]
    ppermute x10 -> x13, starting transfers between devices: 22.8 us -> 25.1 us  [shifted(): return lax.ppermute(value, axis, [(q, (q + by) % n) for q in range(n)])]
    pallas_call x1, Pallas kernels: 9.75 us -> 7.88 us  [grad_outer_of(): pl.pallas_call(lambda *refs: grad_outer_kernel(scale, *refs), grid=(group...]
  transfers between devices with their start and end apart: 18 -> 20, of which waited for: 10 -> 9; matrix products, arithmetic and copies ran while one was open for 6% -> 7% of each run, Pallas kernels for 18% -> 17%
where the time goes in v2:
time: 147 us; the launch traced here: 146 us
  starting transfers between devices  72.3 us (49%)
  Pallas kernels  30.4 us (21%)
  waiting for transfers between devices  23 us (16%)
  local copies, waits for them, and re-layouts  11.8 us (8%)
  other arithmetic  3.97 us (3%)
  matrix products  3.42 us (2%)
    all_to_all x5, starting transfers between devices, exchange(): return lax.all_to_all(pieces, axis, split_axis=0, concat_axis=0, tiled=True)  34.9 us
    ppermute x13, starting transfers between devices, shifted(): return lax.ppermute(value, axis, [(q, (q + by) % n) for q in range(n)])  25.1 us
    ppermute x1, waiting for transfers between devices, step(): left_part = lax.ppermute(left_sum, PLANE, back)  13.2 us
    pallas_call x1, Pallas kernels, outer_of(): pl.pallas_call(lambda *refs: outer_kernel(scale, *refs), grid=(left.shape...  10 us
    ppermute x1, starting transfers between devices, step(): lax.ppermute(left_own.reshape(share, latent * amino), PLANE, there)  7.92 us
    pallas_call x1, Pallas kernels, grad_outer_of(): pl.pallas_call(lambda *refs: grad_outer_kernel(scale, *refs), grid=(group...  7.88 us
    pallas_call x1, Pallas kernels, align_of(): pl.pallas_call(align_kernel, grid=(share // 8,), in_specs=[pl.BlockSpec((...  7.47 us
    ppermute x13, waiting for transfers between devices, shifted(): return lax.ppermute(value, axis, [(q, (q + by) % n) for q in range(n)])  5.25 us
  transfers between devices with their start and end apart: 20, of which 9 were waited for; matrix products, arithmetic and copies ran while one was open for 7% of the time, Pallas kernels for 17%

profile of v2, /device:TPU:1, one launch (start us, length us, event | category | flops | bytes accessed | tf_op | source)
XLA Modules:
  0.0 145.9 jit_solution(3070598053566321963)
XLA Ops:
  0.6 5.1 %panels.1 = (bf16[32,32,96]{2,1,0:T(8,128)(2,1)}, bf16[32,96,32]{2,1,0:T(8,128)(2,1)}) custom-call(bf16[32,96,256]{2,1,0:T(8,128)(2,1)} %align_ref.3, bf16[64,256]{1,0:T(8,128)(2,1)} %bitcast.79), custom_call_target="tpu_custom_call" | custom-call | tf_op jit(solution)/shard_map/panels/pallas_call | solution.py:49
  5.7 1.3 reshape.55
  7.0 7.9 %collective-permute-start = (bf16[32,3072]{1,0:T(8,128)(2,1)S(1)}, bf16[32,3072]{1,0:T(8,128)(2,1)S(1)}, u32[]{:S(2)}, u32[]{:S(2)}) collective-permute-start(bf16[32,3072]{1,0:T(8,128)(2,1)S(1)} %reshape.55), channel_id=1, source_target_pairs={{128,0},{160,4},{64,8},{96,12},{0,16},{32,20},{192,24},{224,28},{1... | collective-permute-start | bytes 589832 | tf_op jit(solution)/shard_map/ppermute | solution.py:241
  14.9 1.6 %reshape.56 = bf16[32,4,768]{2,1,0:T(4,128)(2,1)S(1)} reshape(bf16[32,96,32]{2,1,0:T(8,128)(2,1)} %get-tuple-element.16) | data formatting | bytes 393216 | tf_op jit(solution)/shard_map/reshape | solution.py:242
  16.6 0.7 copy.104
  17.3 4.2 %all-to-all-start = ((bf16[4,32,768]{2,1,0:T(8,128)(2,1)}), bf16[4,32,768]{2,1,0:T(8,128)(2,1)S(1)}, u32[]{:S(2)}, u32[]{:S(2)}) async-start(bf16[4,32,768]{2,1,0:T(8,128)(2,1)} %copy.104), calls=%async_computation | async-start | bytes 393216 | tf_op jit(solution)/shard_map/all_to_all | solution.py:218
  21.4 0.9 copy.128
  22.4 1.5 %collective-permute-start.1 = (bf16[32,3072]{1,0:T(8,128)(2,1)S(1)}, bf16[32,3072]{1,0:T(8,128)(2,1)S(1)}, u32[]{:S(2)}, u32[]{:S(2)}) collective-permute-start(bf16[32,3072]{1,0:T(8,128)(2,1)S(1)} %collective-permute-done), channel_id=1, source_target_pairs={{0,1},{1,2},{2,3},{3,0},{4,5},{5,6},{6,7},{7,4},{8,9},{9,10},{10,1... | collective-permute-start | bytes 589832 | tf_op jit(solution)/shard_map/ppermute | solution.py:205
  23.8 2.4 %collective-permute-start.2 = (bf16[32,3072]{1,0:T(8,128)(2,1)S(1)}, bf16[32,3072]{1,0:T(8,128)(2,1)S(1)}, u32[]{:S(2)}, u32[]{:S(2)}) collective-permute-start(bf16[32,3072]{1,0:T(8,128)(2,1)S(1)} %collective-permute-done), channel_id=1, source_target_pairs={{0,2},{1,3},{2,0},{3,1},{4,6},{5,7},{6,4},{7,5},{8,10},{9,11},{10,... | collective-permute-start | bytes 589832 | tf_op jit(solution)/shard_map/ppermute | solution.py:205
  26.2 1.2 collective-permute-start.3
  27.4 0.7 copy-done.1
  28.1 7.9 %grad_outer.1 = (bf16[3072,768]{1,0:T(8,128)(2,1)}, bf16[128,3072]{1,0:T(8,128)(2,1)}) custom-call(bf16[24,96,128]{2,1,0:T(8,128)(2,1)} %bitcast.65, bf16[1024,128]{1,0:T(8,128)(2,1)} %refs_1_.1, bf16[128,768]{1,0:T(8,128)(2,1)} %bitcast.69), custom_call_target="tpu_custom_call" | custom-call | tf_op jit(solution)/shard_map/grad_outer/pallas_call | solution.py:129
  36.1 3.4 %fusion = bf16[128,768]{1,0:T(8,128)(2,1)S(1)} fusion(bf16[128,3072]{1,0:T(8,128)(2,1)S(1)} %constant_dynamic-update-slice_fusion.refs_0_, bf16[3072,768]{1,0:T(8,128)(2,1)} %get-tuple-element.21), kind=kOutput, calls=%fused_computation.1 | convolution fusion | flops 604176384 | bytes 5701632 | tf_op jit(solution)/shard_map/dot_general | solution.py:257
  39.7 1.0 pad_maximum_fusion
  40.7 3.5 %all-to-all-start.1 = ((bf16[4,32,3840]{2,1,0:T(8,128)(2,1)}), bf16[4,32,3840]{2,1,0:T(8,128)(2,1)S(1)}, u32[]{:S(2)}, u32[]{:S(2)}) async-start(bf16[4,32,3840]{2,1,0:T(8,128)(2,1)} %pad_maximum_fusion), calls=%async_computation.1 | async-start | bytes 1966080 | tf_op jit(solution)/shard_map/all_to_all | solution.py:218
  44.3 0.8 fusion.5
  45.0 10.0 %outer.1 = (bf16[24,96,128]{2,1,0:T(8,128)(2,1)}, bf16[64,24,128]{2,1,0:T(8,128)(2,1)}) custom-call(bf16[128,3072]{1,0:T(8,128)(2,1)} %copy-done, bf16[128,768]{1,0:T(8,128)(2,1)} %bitcast.75, bf16[24,96,128]{2,1,0:T(8,128)(2,1)} %bitcast.66, bf16[1024,128]{1,0:T(8,128)(2,1)} %refs_1_.1, f32[1,128]{1,0:T(1,128)} %bitcast.88), custom_call_target="tpu_custom_call" | custom-call | tf_op jit(solution)/shard_map/outer/pallas_call | solution.py:186
  55.0 0.8 all-to-all-done.1
  56.0 12.1 %all-to-all-start.3 = ((bf16[64,24,128]{2,1,0:T(8,128)(2,1)}), bf16[64,24,128]{2,1,0:T(8,128)(2,1)S(1)}, u32[]{:S(2)}, u32[]{:S(2)}) async-start(bf16[64,24,128]{2,1,0:T(8,128)(2,1)} %get-tuple-element.23), calls=%async_computation.3 | async-start | bytes 786432 | tf_op jit(solution)/shard_map/all_to_all | solution.py:218
  68.0 4.4 %collective-permute-start.4 = (bf16[32,3072]{1,0:T(8,128)(2,1)S(1)}, bf16[32,3072]{1,0:T(8,128)(2,1)S(1)}, u32[]{:S(2)}, u32[]{:S(2)}) collective-permute-start(bf16[32,3072]{1,0:T(8,128)(2,1)S(1)} %slice_reduce_fusion), channel_id=1, source_target_pairs={{0,128},{4,160},{8,64},{12,96},{16,0},{20,32},{24,192},{28,224},{3... | collective-permute-start | bytes 589832 | tf_op jit(solution)/shard_map/ppermute | solution.py:266
  72.6 13.2 %collective-permute-done.4 = bf16[32,3072]{1,0:T(8,128)(2,1)S(1)} collective-permute-done((bf16[32,3072]{1,0:T(8,128)(2,1)S(1)}, bf16[32,3072]{1,0:T(8,128)(2,1)S(1)}, u32[]{:S(2)}, u32[]{:S(2)}) %collective-permute-start.4) | collective-permute-done | bytes 196640 | tf_op jit(solution)/shard_map/ppermute | solution.py:266
  85.9 0.4 fusion.2
  86.3 0.6 fusion.15
  86.9 9.1 %collective-permute-start.10 = (bf16[32,768]{1,0:T(8,128)(2,1)S(1)}, bf16[32,768]{1,0:T(8,128)(2,1)S(1)}, u32[]{:S(2)}, u32[]{:S(2)}) collective-permute-start(bf16[32,768]{1,0:T(8,128)(2,1)S(1)} %bitcast.84), channel_id=1, source_target_pairs={{0,192},{32,224},{64,0},{96,32},{128,64},{160,96},{192,128},{224,1... | collective-permute-start | bytes 147464 | tf_op jit(solution)/shard_map/ppermute | solution.py:205
  96.0 0.4 collective-permute-start.11
  96.4 1.2 collective-permute-start.5
  97.7 0.4 collective-permute-start.6
  98.2 4.8 %collective-permute-start.8 = (bf16[32,768]{1,0:T(8,128)(2,1)S(1)}, bf16[32,768]{1,0:T(8,128)(2,1)S(1)}, u32[]{:S(2)}, u32[]{:S(2)}) collective-permute-start(bf16[32,768]{1,0:T(8,128)(2,1)S(1)} %bitcast.87), channel_id=1, source_target_pairs={{0,128},{32,160},{64,192},{96,224},{128,0},{160,32},{192,64},{224,... | collective-permute-start | bytes 147464 | tf_op jit(solution)/shard_map/ppermute | solution.py:205
  103.0 1.1 collective-permute-done.7
  104.2 0.4 collective-permute-done.8
  104.6 2.3 %collective-permute-done.9 = bf16[32,768]{1,0:T(8,128)(2,1)S(1)} collective-permute-done((bf16[32,768]{1,0:T(8,128)(2,1)S(1)}, bf16[32,768]{1,0:T(8,128)(2,1)S(1)}, u32[]{:S(2)}, u32[]{:S(2)}) %collective-permute-start.9) | collective-permute-done | bytes 49184 | tf_op jit(solution)/shard_map/ppermute | solution.py:205
  107.0 0.8 broadcast_in_dim.4
  107.8 4.8 %all-to-all-start.2 = ((bf16[8,32,768]{2,1,0:T(8,128)(2,1)}), bf16[8,32,768]{2,1,0:T(8,128)(2,1)S(1)}, u32[]{:S(2)}, u32[]{:S(2)}) async-start(bf16[8,32,768]{2,1,0:T(8,128)(2,1)} %broadcast_in_dim.4), calls=%async_computation.2 | async-start | bytes 786432 | tf_op jit(solution)/shard_map/all_to_all | solution.py:218
  112.7 1.4 collective-permute-start.12
  114.1 0.3 collective-permute-start.13
  114.3 2.4 %collective-permute-start.14 = (f32[24,128]{1,0:T(8,128)S(1)}, f32[24,128]{1,0:T(8,128)S(1)}, u32[]{:S(2)}, u32[]{:S(2)}) collective-permute-start(f32[24,128]{1,0:T(8,128)S(1)} %convert_reduce_fusion), channel_id=1, source_target_pairs={{0,3},{1,0},{2,1},{3,2},{4,7},{5,4},{6,5},{7,6},{8,11},{9,8},{10,9... | collective-permute-start | bytes 36872 | tf_op jit(solution)/shard_map/ppermute | solution.py:205
  116.8 1.3 collective-permute-done.13
  118.1 2.6 %all-to-all-done.2 = bf16[8,32,768]{2,1,0:T(8,128)(2,1)S(1)} async-done(((bf16[8,32,768]{2,1,0:T(8,128)(2,1)}), bf16[8,32,768]{2,1,0:T(8,128)(2,1)S(1)}, u32[]{:S(2)}, u32[]{:S(2)}) %all-to-all-start.2) | async-done | bytes 393248 | tf_op jit(solution)/shard_map/all_to_all | solution.py:218
  120.7 0.8 broadcast_in_dim.5
  121.5 10.2 %all-to-all-start.4 = ((bf16[64,16,128]{2,1,0:T(8,128)(2,1)}), bf16[64,16,128]{2,1,0:T(8,128)(2,1)S(1)}, u32[]{:S(2)}, u32[]{:S(2)}) async-start(bf16[64,16,128]{2,1,0:T(8,128)(2,1)} %broadcast_in_dim.5), calls=%async_computation.4 | async-start | bytes 524288 | tf_op jit(solution)/shard_map/all_to_all | solution.py:218
  131.7 1.0 copy.109
  132.8 0.5 slice_bitcast_fusion
  133.3 0.8 reshape.66
  134.3 1.2 copy.108.right_ref
  135.7 0.8 copy.106
  136.5 7.5 %align.1 = f32[32,96,256]{2,1,0:T(8,128)} custom-call(bf16[32,96,256]{2,1,0:T(8,128)(2,1)} %align_ref.3, bf16[32,32,96]{2,1,0:T(8,128)(2,1)} %bitcast.70, bf16[32,96,32]{2,1,0:T(8,128)(2,1)} %copy.108.right_ref, bf16[64,256]{1,0:T(8,128)(2,1)} %bitcast.80), custom_call_target="tpu_custom_call" | custom-call | tf_op jit(solution)/shard_map/align/pallas_call | solution.py:81
  144.0 1.2 all-to-all-done.4
  145.1 0.8 bitcast_convert_fusion
  (51 shorter events, 1.3 us)
Async XLA Ops:
  0.6 20.8 %copy-start.4 = (bf16[96,24,128]{2,1,0:T(8,128)(2,1)S(1)}, bf16[96,24,128]{2,1,0:T(8,128)(2,1)}, u32[]{:S(2)}) copy-start(bf16[96,24,128]{2,1,0:T(8,128)(2,1)} %param.9) | copy-start | bytes 1769476
  7.0 15.4 %collective-permute-start = (bf16[32,3072]{1,0:T(8,128)(2,1)S(1)}, bf16[32,3072]{1,0:T(8,128)(2,1)S(1)}, u32[]{:S(2)}, u32[]{:S(2)}) collective-permute-start(bf16[32,3072]{1,0:T(8,128)(2,1)S(1)} %reshape.55), channel_id=1, source_target_pairs={{128,0},{160,4},{64,8},{96,12},{0,16},{32,20},{192,24},{224,28},{1... | collective-permute-start | bytes 589832 | tf_op jit(solution)/shard_map/ppermute | solution.py:241
  17.3 10.1 %all-to-all-start = ((bf16[4,32,768]{2,1,0:T(8,128)(2,1)}), bf16[4,32,768]{2,1,0:T(8,128)(2,1)S(1)}, u32[]{:S(2)}, u32[]{:S(2)}) async-start(bf16[4,32,768]{2,1,0:T(8,128)(2,1)} %copy.104), calls=%async_computation | async-start | bytes 393216 | tf_op jit(solution)/shard_map/all_to_all | solution.py:218
  22.4 13.6 %collective-permute-start.1 = (bf16[32,3072]{1,0:T(8,128)(2,1)S(1)}, bf16[32,3072]{1,0:T(8,128)(2,1)S(1)}, u32[]{:S(2)}, u32[]{:S(2)}) collective-permute-start(bf16[32,3072]{1,0:T(8,128)(2,1)S(1)} %collective-permute-done), channel_id=1, source_target_pairs={{0,1},{1,2},{2,3},{3,0},{4,5},{5,6},{6,7},{7,4},{8,9},{9,10},{10,1... | collective-permute-start | bytes 589832 | tf_op jit(solution)/shard_map/ppermute | solution.py:205
  23.8 12.2 %collective-permute-start.2 = (bf16[32,3072]{1,0:T(8,128)(2,1)S(1)}, bf16[32,3072]{1,0:T(8,128)(2,1)S(1)}, u32[]{:S(2)}, u32[]{:S(2)}) collective-permute-start(bf16[32,3072]{1,0:T(8,128)(2,1)S(1)} %collective-permute-done), channel_id=1, source_target_pairs={{0,2},{1,3},{2,0},{3,1},{4,6},{5,7},{6,4},{7,5},{8,10},{9,11},{10,... | collective-permute-start | bytes 589832 | tf_op jit(solution)/shard_map/ppermute | solution.py:205
  26.2 9.8 %collective-permute-start.3 = (bf16[32,3072]{1,0:T(8,128)(2,1)S(1)}, bf16[32,3072]{1,0:T(8,128)(2,1)S(1)}, u32[]{:S(2)}, u32[]{:S(2)}) collective-permute-start(bf16[32,3072]{1,0:T(8,128)(2,1)S(1)} %collective-permute-done), channel_id=1, source_target_pairs={{0,3},{1,0},{2,1},{3,2},{4,7},{5,4},{6,5},{7,6},{8,11},{9,8},{10,9... | collective-permute-start | bytes 589832 | tf_op jit(solution)/shard_map/ppermute | solution.py:205
  27.4 0.7 copy-start.1
  36.1 3.6 %copy-start = (bf16[128,3072]{1,0:T(8,128)(2,1)}, bf16[128,3072]{1,0:T(8,128)(2,1)S(1)}, u32[]{:S(2)}) copy-start(bf16[128,3072]{1,0:T(8,128)(2,1)S(1)} %constant_dynamic-update-slice_fusion.refs_0_) | copy-start | bytes 2359300
  36.1 3.6 %copy-start.3 = (bf16[128,3072]{1,0:T(8,128)(2,1)S(1)}, bf16[128,3072]{1,0:T(8,128)(2,1)}, u32[]{:S(2)}) copy-start(bf16[128,3072]{1,0:T(8,128)(2,1)} %get-tuple-element.20) | copy-start | bytes 2359300
  39.5 4.7 %copy-start.2 = (bf16[4,32,768]{2,1,0:T(8,128)(2,1)S(1)}, bf16[4,32,768]{2,1,0:T(8,128)(2,1)}, u32[]{:S(2)}) copy-start(bf16[4,32,768]{2,1,0:T(8,128)(2,1)} %copy-done.1) | copy-start | bytes 589828
  40.7 15.1 %all-to-all-start.1 = ((bf16[4,32,3840]{2,1,0:T(8,128)(2,1)}), bf16[4,32,3840]{2,1,0:T(8,128)(2,1)S(1)}, u32[]{:S(2)}, u32[]{:S(2)}) async-start(bf16[4,32,3840]{2,1,0:T(8,128)(2,1)} %pad_maximum_fusion), calls=%async_computation.1 | async-start | bytes 1966080 | tf_op jit(solution)/shard_map/all_to_all | solution.py:218
  56.0 51.0 %all-to-all-start.3 = ((bf16[64,24,128]{2,1,0:T(8,128)(2,1)}), bf16[64,24,128]{2,1,0:T(8,128)(2,1)S(1)}, u32[]{:S(2)}, u32[]{:S(2)}) async-start(bf16[64,24,128]{2,1,0:T(8,128)(2,1)} %get-tuple-element.23), calls=%async_computation.3 | async-start | bytes 786432 | tf_op jit(solution)/shard_map/all_to_all | solution.py:218
  68.0 17.8 %collective-permute-start.4 = (bf16[32,3072]{1,0:T(8,128)(2,1)S(1)}, bf16[32,3072]{1,0:T(8,128)(2,1)S(1)}, u32[]{:S(2)}, u32[]{:S(2)}) collective-permute-start(bf16[32,3072]{1,0:T(8,128)(2,1)S(1)} %slice_reduce_fusion), channel_id=1, source_target_pairs={{0,128},{4,160},{8,64},{12,96},{16,0},{20,32},{24,192},{28,224},{3... | collective-permute-start | bytes 589832 | tf_op jit(solution)/shard_map/ppermute | solution.py:266
  85.9 45.8 %copy-start.5 = (bf16[24,96,128]{2,1,0:T(8,128)(2,1)S(1)}, bf16[24,96,128]{2,1,0:T(8,128)(2,1)}, u32[]{:S(2)}) copy-start(bf16[24,96,128]{2,1,0:T(8,128)(2,1)} %get-tuple-element.18) | copy-start | bytes 1769476
  86.9 11.3 %collective-permute-start.10 = (bf16[32,768]{1,0:T(8,128)(2,1)S(1)}, bf16[32,768]{1,0:T(8,128)(2,1)S(1)}, u32[]{:S(2)}, u32[]{:S(2)}) collective-permute-start(bf16[32,768]{1,0:T(8,128)(2,1)S(1)} %bitcast.84), channel_id=1, source_target_pairs={{0,192},{32,224},{64,0},{96,32},{128,64},{160,96},{192,128},{224,1... | collective-permute-start | bytes 147464 | tf_op jit(solution)/shard_map/ppermute | solution.py:205
  96.0 7.0 %collective-permute-start.11 = (bf16[32,768]{1,0:T(8,128)(2,1)S(1)}, bf16[32,768]{1,0:T(8,128)(2,1)S(1)}, u32[]{:S(2)}, u32[]{:S(2)}) collective-permute-start(bf16[32,768]{1,0:T(8,128)(2,1)S(1)} %bitcast.82), channel_id=1, source_target_pairs={{0,224},{32,0},{64,32},{96,64},{128,96},{160,128},{192,160},{224,1... | collective-permute-start | bytes 147464 | tf_op jit(solution)/shard_map/ppermute | solution.py:205
  96.4 6.6 %collective-permute-start.5 = (bf16[32,768]{1,0:T(8,128)(2,1)S(1)}, bf16[32,768]{1,0:T(8,128)(2,1)S(1)}, u32[]{:S(2)}, u32[]{:S(2)}) collective-permute-start(bf16[32,768]{1,0:T(8,128)(2,1)S(1)} %bitcast.81), channel_id=1, source_target_pairs={{0,32},{32,64},{64,96},{96,128},{128,160},{160,192},{192,224},{224... | collective-permute-start | bytes 147464 | tf_op jit(solution)/shard_map/ppermute | solution.py:205
  97.7 5.4 %collective-permute-start.6 = (bf16[32,768]{1,0:T(8,128)(2,1)S(1)}, bf16[32,768]{1,0:T(8,128)(2,1)S(1)}, u32[]{:S(2)}, u32[]{:S(2)}) collective-permute-start(bf16[32,768]{1,0:T(8,128)(2,1)S(1)} %bitcast.83), channel_id=1, source_target_pairs={{0,64},{32,96},{64,128},{96,160},{128,192},{160,224},{192,0},{224,... | collective-permute-start | bytes 147464 | tf_op jit(solution)/shard_map/ppermute | solution.py:205
  98.1 6.1 %collective-permute-start.7 = (bf16[32,768]{1,0:T(8,128)(2,1)S(1)}, bf16[32,768]{1,0:T(8,128)(2,1)S(1)}, u32[]{:S(2)}, u32[]{:S(2)}) collective-permute-start(bf16[32,768]{1,0:T(8,128)(2,1)S(1)} %bitcast.85), channel_id=1, source_target_pairs={{0,96},{32,128},{64,160},{96,192},{128,224},{160,0},{192,32},{224,... | collective-permute-start | bytes 147464 | tf_op jit(solution)/shard_map/ppermute | solution.py:205
  98.2 6.3 %collective-permute-start.8 = (bf16[32,768]{1,0:T(8,128)(2,1)S(1)}, bf16[32,768]{1,0:T(8,128)(2,1)S(1)}, u32[]{:S(2)}, u32[]{:S(2)}) collective-permute-start(bf16[32,768]{1,0:T(8,128)(2,1)S(1)} %bitcast.87), channel_id=1, source_target_pairs={{0,128},{32,160},{64,192},{96,224},{128,0},{160,32},{192,64},{224,... | collective-permute-start | bytes 147464 | tf_op jit(solution)/shard_map/ppermute | solution.py:205
  103.0 3.9 %collective-permute-start.9 = (bf16[32,768]{1,0:T(8,128)(2,1)S(1)}, bf16[32,768]{1,0:T(8,128)(2,1)S(1)}, u32[]{:S(2)}, u32[]{:S(2)}) collective-permute-start(bf16[32,768]{1,0:T(8,128)(2,1)S(1)} %bitcast.86), channel_id=1, source_target_pairs={{0,160},{32,192},{64,224},{96,0},{128,32},{160,64},{192,96},{224,1... | collective-permute-start | bytes 147464 | tf_op jit(solution)/shard_map/ppermute | solution.py:205
  107.8 12.9 %all-to-all-start.2 = ((bf16[8,32,768]{2,1,0:T(8,128)(2,1)}), bf16[8,32,768]{2,1,0:T(8,128)(2,1)S(1)}, u32[]{:S(2)}, u32[]{:S(2)}) async-start(bf16[8,32,768]{2,1,0:T(8,128)(2,1)} %broadcast_in_dim.4), calls=%async_computation.2 | async-start | bytes 786432 | tf_op jit(solution)/shard_map/all_to_all | solution.py:218
  112.7 4.1 %collective-permute-start.12 = (f32[24,128]{1,0:T(8,128)S(1)}, f32[24,128]{1,0:T(8,128)S(1)}, u32[]{:S(2)}, u32[]{:S(2)}) collective-permute-start(f32[24,128]{1,0:T(8,128)S(1)} %convert_reduce_fusion), channel_id=1, source_target_pairs={{0,2},{1,3},{2,0},{3,1},{4,6},{5,7},{6,4},{7,5},{8,10},{9,11},{10,... | collective-permute-start | bytes 36872 | tf_op jit(solution)/shard_map/ppermute | solution.py:205
  114.1 4.1 %collective-permute-start.13 = (f32[24,128]{1,0:T(8,128)S(1)}, f32[24,128]{1,0:T(8,128)S(1)}, u32[]{:S(2)}, u32[]{:S(2)}) collective-permute-start(f32[24,128]{1,0:T(8,128)S(1)} %convert_reduce_fusion), channel_id=1, source_target_pairs={{0,1},{1,2},{2,3},{3,0},{4,5},{5,6},{6,7},{7,4},{8,9},{9,10},{10,1... | collective-permute-start | bytes 36872 | tf_op jit(solution)/shard_map/ppermute | solution.py:205
  114.3 3.8 %collective-permute-start.14 = (f32[24,128]{1,0:T(8,128)S(1)}, f32[24,128]{1,0:T(8,128)S(1)}, u32[]{:S(2)}, u32[]{:S(2)}) collective-permute-start(f32[24,128]{1,0:T(8,128)S(1)} %convert_reduce_fusion), channel_id=1, source_target_pairs={{0,3},{1,0},{2,1},{3,2},{4,7},{5,4},{6,5},{7,6},{8,11},{9,8},{10,9... | collective-permute-start | bytes 36872 | tf_op jit(solution)/shard_map/ppermute | solution.py:205
  121.5 23.7 %all-to-all-start.4 = ((bf16[64,16,128]{2,1,0:T(8,128)(2,1)}), bf16[64,16,128]{2,1,0:T(8,128)(2,1)S(1)}, u32[]{:S(2)}, u32[]{:S(2)}) async-start(bf16[64,16,128]{2,1,0:T(8,128)(2,1)} %broadcast_in_dim.5), calls=%async_computation.4 | async-start | bytes 524288 | tf_op jit(solution)/shard_map/all_to_all | solution.py:218

commit v3 on v2

--- a/solution.py
+++ b/solution.py
@@ -14,13 +14,7 @@
 
 
 def lane_mean(values):
-    share = jnp.full((values.shape[-1], 128), 1.0 / values.shape[-1], BF)
-    high = values.astype(BF)
-    mean = jnp.dot(high, share, preferred_element_type=F32)
-    if values.dtype == F32:
-        low = (values - high.astype(F32)).astype(BF)
-        mean = mean + jnp.dot(low, share, preferred_element_type=F32)
-    return jnp.concatenate([mean, mean], axis=-1)
+    return jnp.mean(values.astype(F32), axis=-1, keepdims=True)
 
 
 def standardized(rows):
@@ -58,6 +52,7 @@
             jax.ShapeDtypeStruct((share, latent, amino), BF),
             jax.ShapeDtypeStruct((share, amino, latent), BF),
         ],
+        compiler_params=pltpu.CompilerParams(vmem_limit_bytes=24 << 20),
         name="panels",
     )(align, weights)
 
@@ -89,6 +84,7 @@
         ],
         out_specs=pl.BlockSpec((8, amino, width), lambda g: (g, 0, 0)),
         out_shape=jax.ShapeDtypeStruct(align.shape, F32),
+        compiler_params=pltpu.CompilerParams(vmem_limit_bytes=24 << 20),
         name="align",
     )(align, left_grad, right_grad, weights)
 
@@ -110,6 +106,7 @@
 def grad_outer_kernel(scale, adj_ref, final_ref, right_ref, outer_ref, left_ref):
     quarter, block_i, width = adj_ref.shape
     final = final_ref[...]
+    outer_ref = outer_ref.at[pl.ds(pl.program_id(0) * 8 * block_i, 8 * block_i)]
     for four in range(quarter // 4):
         adj = adj_ref[four * 4 : (four + 1) * 4].reshape(4 * block_i, width)
         g = lax.dot_general(adj, final, NT, preferred_element_type=F32).astype(BF)
@@ -135,13 +132,14 @@
             pl.BlockSpec(right.shape, lambda g: (0, 0)),
         ],
         out_specs=[
-            pl.BlockSpec((8 * block_i, lanes), lambda g: (g, 0)),
+            pl.BlockSpec(memory_space=pltpu.VMEM),
             pl.BlockSpec((seqs, 8 * block_i), lambda g: (0, g)),
         ],
         out_shape=[
-            jax.ShapeDtypeStruct((groups * 8 * block_i, lanes), BF),
+            pltpu.VMEM((groups * 8 * block_i, lanes), BF),
             jax.ShapeDtypeStruct((seqs, groups * 8 * block_i), BF),
         ],
+        compiler_params=pltpu.CompilerParams(vmem_limit_bytes=24 << 20),
         name="grad_outer",
     )(adj, final, right)
 
@@ -196,6 +194,7 @@
         out_specs=[whole(adj.shape), whole(weight)],
         out_shape=[jax.ShapeDtypeStruct(adj.shape, BF), jax.ShapeDtypeStruct(weight, BF)],
         scratch_shapes=[pltpu.VMEM((quarter * block_i, final.shape[0]), BF)],
+        compiler_params=pltpu.CompilerParams(vmem_limit_bytes=24 << 20),
         name="outer",
     )(left, right, adj, final, offset.reshape(1, width))
 
@@ -285,6 +284,7 @@
     received = exchange(weight, PLANE)
     mine = jnp.sum(received.astype(F32), axis=0)
     total = ((mine + shifted(mine, "depth", 2)) + (shifted(mine, "depth", 1) + shifted(mine, "depth", 3))) / crop_length
+    total, contact_delta = lax.optimization_barrier((total, contact_delta))
     weight_gradient = exchange(copies(total[:rows].astype(BF), plane_count), PLANE)
     weight_gradient = weight_gradient.reshape(kron, width).astype(F32)
     return contact_delta, alignment_adjoint, weight_gradient, total[rows]

time: 147 us -> 126 us (0.86)
  Pallas kernels: 30.4 us -> 20 us
  starting transfers between devices: 72.3 us -> 67.9 us
  matrix products: 3.42 us -> 0.79 us
  local copies, waits for them, and re-layouts: 11.8 us -> 9.61 us
  waiting for transfers between devices: 23 us -> 21.4 us
    ppermute x1, waiting for transfers between devices: 13.2 us -> 0.01 us  [step(): left_part = lax.ppermute(left_sum, PLANE, back)]
    all_to_all x5, waiting for transfers between devices: 4.55 us -> 14.2 us  [exchange(): return lax.all_to_all(pieces, axis, split_axis=0, concat_axis=0, tiled=True)]
    pallas_call x1, Pallas kernels: 7.47 us -> 3.88 us  [align_of(): pl.pallas_call(align_kernel, grid=(share // 8,), in_specs=[pl.BlockSpec((...]
    ppermute x1, starting transfers between devices: 4.45 us -> 1.2 us  [step(): left_part = lax.ppermute(left_sum, PLANE, back)]
    dot_general x1, matrix products: 3.42 us -> 0.79 us  [step(): lax.dot_general(left, grad_outer, (((1,), (0,)), ((), ())), preferred_ele...]
    pallas_call x1, Pallas kernels: 5.07 us -> 2.63 us  [panels_of(): pl.pallas_call(panels_kernel, grid=(share // 8,), in_specs=[pl.BlockSpec(...]
    pallas_call x1, Pallas kernels: 10 us -> 7.69 us  [outer_of(): pl.pallas_call(lambda *refs: outer_kernel(scale, *refs), grid=(left.shape...]
    pallas_call x1, Pallas kernels: 7.88 us -> 5.81 us  [grad_outer_of(): pl.pallas_call(lambda *refs: grad_outer_kernel(scale, *refs), grid=(group...]
  transfers between devices with their start and end apart: 20 -> 20, of which waited for: 9 -> 11; matrix products, arithmetic and copies ran while one was open for 7% -> 5% of each run, Pallas kernels for 17% -> 14%
where the time goes in v3:
time: 126 us; the launch traced here: 125 us
  starting transfers between devices  67.9 us (54%)
  waiting for transfers between devices  21.4 us (17%)
  Pallas kernels  20 us (16%)
  local copies, waits for them, and re-layouts  9.61 us (8%)
  other arithmetic  4.43 us (4%)
    all_to_all x5, starting transfers between devices, exchange(): return lax.all_to_all(pieces, axis, split_axis=0, concat_axis=0, tiled=True)  32.9 us
    ppermute x13, starting transfers between devices, shifted(): return lax.ppermute(value, axis, [(q, (q + by) % n) for q in range(n)])  25.8 us
    all_to_all x5, waiting for transfers between devices, exchange(): return lax.all_to_all(pieces, axis, split_axis=0, concat_axis=0, tiled=True)  14.2 us
    ppermute x1, starting transfers between devices, step(): lax.ppermute(left_own.reshape(share, latent * amino), PLANE, there)  7.92 us
    pallas_call x1, Pallas kernels, outer_of(): pl.pallas_call(lambda *refs: outer_kernel(scale, *refs), grid=(left.shape...  7.69 us
    ppermute x13, waiting for transfers between devices, shifted(): return lax.ppermute(value, axis, [(q, (q + by) % n) for q in range(n)])  7.19 us
    pallas_call x1, Pallas kernels, grad_outer_of(): pl.pallas_call(lambda *refs: grad_outer_kernel(scale, *refs), grid=(group...  5.81 us
    pallas_call x1, Pallas kernels, align_of(): pl.pallas_call(align_kernel, grid=(share // 8,), in_specs=[pl.BlockSpec((...  3.88 us
  transfers between devices with their start and end apart: 20, of which 11 were waited for; matrix products, arithmetic and copies ran while one was open for 5% of the time, Pallas kernels for 14%

profile of v3, /device:TPU:1, one launch (start us, length us, event | category | flops | bytes accessed | tf_op | source)
XLA Modules:
  0.0 125.1 jit_solution(1566047032694196335)
XLA Ops:
  0.6 1.4 %copy-done = bf16[32,96,256]{2,1,0:T(8,128)(2,1)S(1)} copy-done((bf16[32,96,256]{2,1,0:T(8,128)(2,1)S(1)}, bf16[32,96,256]{2,1,0:T(8,128)(2,1)}, u32[]{:S(2)}) %copy-start) | copy-done | bytes 1572888
  2.0 0.8 copy-done.3
  2.8 2.6 %panels.1 = (bf16[32,32,96]{2,1,0:T(8,128)(2,1)S(1)}, bf16[32,96,32]{2,1,0:T(8,128)(2,1)S(1)}) custom-call(bf16[32,96,256]{2,1,0:T(8,128)(2,1)S(1)} %copy-done, bf16[64,256]{1,0:T(8,128)(2,1)S(1)} %bitcast.72), custom_call_target="tpu_custom_call" | custom-call | tf_op jit(solution)/shard_map/panels/pallas_call | solution.py:43
  5.4 0.3 reshape.55
  5.8 7.9 %collective-permute-start = (bf16[32,3072]{1,0:T(8,128)(2,1)S(1)}, bf16[32,3072]{1,0:T(8,128)(2,1)S(1)}, u32[]{:S(2)}, u32[]{:S(2)}) collective-permute-start(bf16[32,3072]{1,0:T(8,128)(2,1)S(1)} %reshape.55), channel_id=1, source_target_pairs={{128,0},{160,4},{64,8},{96,12},{0,16},{32,20},{192,24},{224,28},{1... | collective-permute-start | bytes 589832 | tf_op jit(solution)/shard_map/ppermute | solution.py:240
  13.7 0.4 reshape.56
  14.1 0.7 copy.104
  14.8 4.2 %all-to-all-start = ((bf16[4,32,768]{2,1,0:T(8,128)(2,1)}), bf16[4,32,768]{2,1,0:T(8,128)(2,1)S(1)}, u32[]{:S(2)}, u32[]{:S(2)}) async-start(bf16[4,32,768]{2,1,0:T(8,128)(2,1)} %copy.104), calls=%async_computation | async-start | bytes 393216 | tf_op jit(solution)/shard_map/all_to_all | solution.py:217
  19.1 1.5 %collective-permute-start.1 = (bf16[32,3072]{1,0:T(8,128)(2,1)S(1)}, bf16[32,3072]{1,0:T(8,128)(2,1)S(1)}, u32[]{:S(2)}, u32[]{:S(2)}) collective-permute-start(bf16[32,3072]{1,0:T(8,128)(2,1)S(1)} %collective-permute-done), channel_id=1, source_target_pairs={{0,1},{1,2},{2,3},{3,0},{4,5},{5,6},{6,7},{7,4},{8,9},{9,10},{10,1... | collective-permute-start | bytes 589832 | tf_op jit(solution)/shard_map/ppermute | solution.py:204
  20.7 2.4 %collective-permute-start.2 = (bf16[32,3072]{1,0:T(8,128)(2,1)S(1)}, bf16[32,3072]{1,0:T(8,128)(2,1)S(1)}, u32[]{:S(2)}, u32[]{:S(2)}) collective-permute-start(bf16[32,3072]{1,0:T(8,128)(2,1)S(1)} %collective-permute-done), channel_id=1, source_target_pairs={{0,2},{1,3},{2,0},{3,1},{4,6},{5,7},{6,4},{7,5},{8,10},{9,11},{10,... | collective-permute-start | bytes 589832 | tf_op jit(solution)/shard_map/ppermute | solution.py:204
  23.1 1.2 collective-permute-start.3
  24.3 5.8 %grad_outer.1 = (bf16[3072,768]{1,0:T(8,128)(2,1)S(1)}, bf16[128,3072]{1,0:T(8,128)(2,1)S(1)}) custom-call(bf16[24,96,128]{2,1,0:T(8,128)(2,1)S(1)} %bitcast.65, bf16[1024,128]{1,0:T(8,128)(2,1)S(1)} %copy-done.2, bf16[128,768]{1,0:T(8,128)(2,1)S(1)} %bitcast.67), custom_call_target="tpu_custom_call" | custom-call | tf_op jit(solution)/shard_map/grad_outer/pallas_call | solution.py:126
  30.2 2.2 %collective-permute-done.2 = bf16[32,3072]{1,0:T(8,128)(2,1)S(1)} collective-permute-done((bf16[32,3072]{1,0:T(8,128)(2,1)S(1)}, bf16[32,3072]{1,0:T(8,128)(2,1)S(1)}, u32[]{:S(2)}, u32[]{:S(2)}) %collective-permute-start.2) | collective-permute-done | bytes 196640 | tf_op jit(solution)/shard_map/ppermute | solution.py:204
  32.5 0.8 fusion
  33.4 1.0 pad_maximum_fusion
  34.4 4.2 %all-to-all-start.1 = ((bf16[4,32,3840]{2,1,0:T(8,128)(2,1)}), bf16[4,32,3840]{2,1,0:T(8,128)(2,1)}, u32[]{:S(2)}, u32[]{:S(2)}) async-start(bf16[4,32,3840]{2,1,0:T(8,128)(2,1)} %pad_maximum_fusion), calls=%async_computation.1 | async-start | bytes 1966080 | tf_op jit(solution)/shard_map/all_to_all | solution.py:217
  38.8 7.7 %outer.1 = (bf16[24,96,128]{2,1,0:T(8,128)(2,1)S(1)}, bf16[64,24,128]{2,1,0:T(8,128)(2,1)}) custom-call(bf16[128,3072]{1,0:T(8,128)(2,1)S(1)} %constant_dynamic-update-slice_fusion.refs_0_, bf16[128,768]{1,0:T(8,128)(2,1)S(1)} %bitcast.70, bf16[24,96,128]{2,1,0:T(8,128)(2,1)S(1)} %bitcast.66, bf16[1024,128]{1,0:T(8,128)(2,1)S(1)} %copy-done.2, ...), custom_call_target="tpu_custom_call" | custom-call | tf_op jit(solution)/shard_map/outer/pallas_call | solution.py:184
  46.5 4.7 %all-to-all-done.1 = bf16[4,32,3840]{2,1,0:T(8,128)(2,1)} async-done(((bf16[4,32,3840]{2,1,0:T(8,128)(2,1)}), bf16[4,32,3840]{2,1,0:T(8,128)(2,1)}, u32[]{:S(2)}, u32[]{:S(2)}) %all-to-all-start.1) | async-done | bytes 983072 | tf_op jit(solution)/shard_map/all_to_all | solution.py:217
  51.2 1.2 slice_reduce_fusion
  52.5 1.2 collective-permute-start.7
  53.7 13.9 %all-to-all-start.2 = ((bf16[64,24,128]{2,1,0:T(8,128)(2,1)}), bf16[64,24,128]{2,1,0:T(8,128)(2,1)S(1)}, u32[]{:S(2)}, u32[]{:S(2)}) async-start(bf16[64,24,128]{2,1,0:T(8,128)(2,1)} %get-tuple-element.23), calls=%async_computation.2 | async-start | bytes 786432 | tf_op jit(solution)/shard_map/all_to_all | solution.py:217
  67.6 1.0 fusion.13
  68.7 0.4 fusion.2
  69.1 0.6 fusion.15
  69.7 3.1 %collective-permute-start.10 = (bf16[32,768]{1,0:T(8,128)(2,1)S(1)}, bf16[32,768]{1,0:T(8,128)(2,1)S(1)}, u32[]{:S(2)}, u32[]{:S(2)}) collective-permute-start(bf16[32,768]{1,0:T(8,128)(2,1)S(1)} %bitcast.85), channel_id=1, source_target_pairs={{0,96},{32,128},{64,160},{96,192},{128,224},{160,0},{192,32},{224,... | collective-permute-start | bytes 147464 | tf_op jit(solution)/shard_map/ppermute | solution.py:204
  72.9 10.0 %collective-permute-start.11 = (bf16[32,768]{1,0:T(8,128)(2,1)S(1)}, bf16[32,768]{1,0:T(8,128)(2,1)S(1)}, u32[]{:S(2)}, u32[]{:S(2)}) collective-permute-start(bf16[32,768]{1,0:T(8,128)(2,1)S(1)} %bitcast.83), channel_id=1, source_target_pairs={{0,128},{32,160},{64,192},{96,224},{128,0},{160,32},{192,64},{224,... | collective-permute-start | bytes 147464 | tf_op jit(solution)/shard_map/ppermute | solution.py:204
  82.9 2.0 %collective-permute-start.13 = (bf16[32,768]{1,0:T(8,128)(2,1)S(1)}, bf16[32,768]{1,0:T(8,128)(2,1)S(1)}, u32[]{:S(2)}, u32[]{:S(2)}) collective-permute-start(bf16[32,768]{1,0:T(8,128)(2,1)S(1)} %bitcast.84), channel_id=1, source_target_pairs={{0,192},{32,224},{64,0},{96,32},{128,64},{160,96},{192,128},{224,1... | collective-permute-start | bytes 147464 | tf_op jit(solution)/shard_map/ppermute | solution.py:204
  85.1 1.5 %collective-permute-start.8 = (bf16[32,768]{1,0:T(8,128)(2,1)S(1)}, bf16[32,768]{1,0:T(8,128)(2,1)S(1)}, u32[]{:S(2)}, u32[]{:S(2)}) collective-permute-start(bf16[32,768]{1,0:T(8,128)(2,1)S(1)} %bitcast.88), channel_id=1, source_target_pairs={{0,32},{32,64},{64,96},{96,128},{128,160},{160,192},{192,224},{224... | collective-permute-start | bytes 147464 | tf_op jit(solution)/shard_map/ppermute | solution.py:204
  86.7 0.6 collective-permute-start.9
  87.2 0.3 collective-permute-done.13
  87.6 0.7 collective-permute-done.14
  88.3 1.9 %collective-permute-done.8 = bf16[32,768]{1,0:T(8,128)(2,1)S(1)} collective-permute-done((bf16[32,768]{1,0:T(8,128)(2,1)S(1)}, bf16[32,768]{1,0:T(8,128)(2,1)S(1)}, u32[]{:S(2)}, u32[]{:S(2)}) %collective-permute-start.8) | collective-permute-done | bytes 49184 | tf_op jit(solution)/shard_map/ppermute | solution.py:204
  90.3 0.6 collective-permute-done.9
  90.9 0.8 broadcast_in_dim.4
  91.7 3.5 %all-to-all-start.3 = ((bf16[8,32,768]{2,1,0:T(8,128)(2,1)}), bf16[8,32,768]{2,1,0:T(8,128)(2,1)S(1)}, u32[]{:S(2)}, u32[]{:S(2)}) async-start(bf16[8,32,768]{2,1,0:T(8,128)(2,1)} %broadcast_in_dim.4), calls=%async_computation.3 | async-start | bytes 786432 | tf_op jit(solution)/shard_map/all_to_all | solution.py:217
  95.2 0.7 collective-permute-start.4
  95.8 1.2 collective-permute-start.5
  97.1 1.5 %collective-permute-start.6 = (f32[24,128]{1,0:T(8,128)S(1)}, f32[24,128]{1,0:T(8,128)S(1)}, u32[]{:S(2)}, u32[]{:S(2)}) collective-permute-start(f32[24,128]{1,0:T(8,128)S(1)} %convert_reduce_fusion), channel_id=1, source_target_pairs={{0,3},{1,0},{2,1},{3,2},{4,7},{5,4},{6,5},{7,6},{8,11},{9,8},{10,9... | collective-permute-start | bytes 36872 | tf_op jit(solution)/shard_map/ppermute | solution.py:204
  98.5 1.1 collective-permute-done.4
  99.9 3.1 %all-to-all-done.3 = bf16[8,32,768]{2,1,0:T(8,128)(2,1)S(1)} async-done(((bf16[8,32,768]{2,1,0:T(8,128)(2,1)}), bf16[8,32,768]{2,1,0:T(8,128)(2,1)S(1)}, u32[]{:S(2)}, u32[]{:S(2)}) %all-to-all-start.3) | async-done | bytes 393248 | tf_op jit(solution)/shard_map/all_to_all | solution.py:217
  103.0 0.7 broadcast_in_dim.5
  103.8 7.1 %all-to-all-start.4 = ((bf16[64,16,128]{2,1,0:T(8,128)(2,1)}), bf16[64,16,128]{2,1,0:T(8,128)(2,1)S(1)}, u32[]{:S(2)}, u32[]{:S(2)}) async-start(bf16[64,16,128]{2,1,0:T(8,128)(2,1)} %broadcast_in_dim.5), calls=%async_computation.4 | async-start | bytes 524288 | tf_op jit(solution)/shard_map/all_to_all | solution.py:217
  110.9 1.0 copy.109
  111.9 0.5 slice_bitcast_fusion
  112.5 0.8 reshape.66
  114.1 3.9 %align.1 = f32[32,96,256]{2,1,0:T(8,128)} custom-call(bf16[32,96,256]{2,1,0:T(8,128)(2,1)S(1)} %copy-done.1, bf16[32,32,96]{2,1,0:T(8,128)(2,1)S(1)} %bitcast.68, bf16[32,96,32]{2,1,0:T(8,128)(2,1)S(1)} %copy.108.right_ref, bf16[64,256]{1,0:T(8,128)(2,1)S(1)} %bitcast.73), custom_call_target="tpu_custom_call" | custom-call | tf_op jit(solution)/shard_map/align/pallas_call | solution.py:76
  118.0 6.3 %all-to-all-done.4 = bf16[64,16,128]{2,1,0:T(8,128)(2,1)S(1)} async-done(((bf16[64,16,128]{2,1,0:T(8,128)(2,1)}), bf16[64,16,128]{2,1,0:T(8,128)(2,1)S(1)}, u32[]{:S(2)}, u32[]{:S(2)}) %all-to-all-start.4) | async-done | bytes 262176 | tf_op jit(solution)/shard_map/all_to_all | solution.py:217
  124.3 0.8 bitcast_convert_fusion
  (53 shorter events, 2.1 us)
Async XLA Ops:
  0.6 1.4 %copy-start = (bf16[32,96,256]{2,1,0:T(8,128)(2,1)S(1)}, bf16[32,96,256]{2,1,0:T(8,128)(2,1)}, u32[]{:S(2)}) copy-start(bf16[32,96,256]{2,1,0:T(8,128)(2,1)} %align_ref.3) | copy-start | bytes 4718596
  2.0 0.8 copy-start.3
  2.8 16.2 %copy-start.6 = (bf16[96,24,128]{2,1,0:T(8,128)(2,1)S(1)}, bf16[96,24,128]{2,1,0:T(8,128)(2,1)}, u32[]{:S(2)}) copy-start(bf16[96,24,128]{2,1,0:T(8,128)(2,1)} %param.9) | copy-start | bytes 1769476
  2.8 21.5 %copy-start.2 = (bf16[1024,128]{1,0:T(8,128)(2,1)S(1)}, bf16[1024,128]{1,0:T(8,128)(2,1)}, u32[]{:S(2)}) copy-start(bf16[1024,128]{1,0:T(8,128)(2,1)} %refs_1_.1) | copy-start | bytes 786436
  5.8 13.4 %collective-permute-start = (bf16[32,3072]{1,0:T(8,128)(2,1)S(1)}, bf16[32,3072]{1,0:T(8,128)(2,1)S(1)}, u32[]{:S(2)}, u32[]{:S(2)}) collective-permute-start(bf16[32,3072]{1,0:T(8,128)(2,1)S(1)} %reshape.55), channel_id=1, source_target_pairs={{128,0},{160,4},{64,8},{96,12},{0,16},{32,20},{192,24},{224,28},{1... | collective-permute-start | bytes 589832 | tf_op jit(solution)/shard_map/ppermute | solution.py:240
  14.8 9.5 %all-to-all-start = ((bf16[4,32,768]{2,1,0:T(8,128)(2,1)}), bf16[4,32,768]{2,1,0:T(8,128)(2,1)S(1)}, u32[]{:S(2)}, u32[]{:S(2)}) async-start(bf16[4,32,768]{2,1,0:T(8,128)(2,1)} %copy.104), calls=%async_computation | async-start | bytes 393216 | tf_op jit(solution)/shard_map/all_to_all | solution.py:217
  19.1 11.0 %collective-permute-start.1 = (bf16[32,3072]{1,0:T(8,128)(2,1)S(1)}, bf16[32,3072]{1,0:T(8,128)(2,1)S(1)}, u32[]{:S(2)}, u32[]{:S(2)}) collective-permute-start(bf16[32,3072]{1,0:T(8,128)(2,1)S(1)} %collective-permute-done), channel_id=1, source_target_pairs={{0,1},{1,2},{2,3},{3,0},{4,5},{5,6},{6,7},{7,4},{8,9},{9,10},{10,1... | collective-permute-start | bytes 589832 | tf_op jit(solution)/shard_map/ppermute | solution.py:204
  20.7 11.7 %collective-permute-start.2 = (bf16[32,3072]{1,0:T(8,128)(2,1)S(1)}, bf16[32,3072]{1,0:T(8,128)(2,1)S(1)}, u32[]{:S(2)}, u32[]{:S(2)}) collective-permute-start(bf16[32,3072]{1,0:T(8,128)(2,1)S(1)} %collective-permute-done), channel_id=1, source_target_pairs={{0,2},{1,3},{2,0},{3,1},{4,6},{5,7},{6,4},{7,5},{8,10},{9,11},{10,... | collective-permute-start | bytes 589832 | tf_op jit(solution)/shard_map/ppermute | solution.py:204
  23.1 9.3 %collective-permute-start.3 = (bf16[32,3072]{1,0:T(8,128)(2,1)S(1)}, bf16[32,3072]{1,0:T(8,128)(2,1)S(1)}, u32[]{:S(2)}, u32[]{:S(2)}) collective-permute-start(bf16[32,3072]{1,0:T(8,128)(2,1)S(1)} %collective-permute-done), channel_id=1, source_target_pairs={{0,3},{1,0},{2,1},{3,2},{4,7},{5,4},{6,5},{7,6},{8,11},{9,8},{10,9... | collective-permute-start | bytes 589832 | tf_op jit(solution)/shard_map/ppermute | solution.py:204
  33.3 5.5 %copy-start.5 = (f32[128]{0:T(128)S(1)}, f32[128]{0:T(128)}, u32[]{:S(2)}) copy-start(f32[128]{0:T(128)} %param.8) | copy-start | bytes 1540
  34.4 16.8 %all-to-all-start.1 = ((bf16[4,32,3840]{2,1,0:T(8,128)(2,1)}), bf16[4,32,3840]{2,1,0:T(8,128)(2,1)}, u32[]{:S(2)}, u32[]{:S(2)}) async-start(bf16[4,32,3840]{2,1,0:T(8,128)(2,1)} %pad_maximum_fusion), calls=%async_computation.1 | async-start | bytes 1966080 | tf_op jit(solution)/shard_map/all_to_all | solution.py:217
  52.5 16.2 %collective-permute-start.7 = (bf16[32,3072]{1,0:T(8,128)(2,1)S(1)}, bf16[32,3072]{1,0:T(8,128)(2,1)S(1)}, u32[]{:S(2)}, u32[]{:S(2)}) collective-permute-start(bf16[32,3072]{1,0:T(8,128)(2,1)S(1)} %slice_reduce_fusion), channel_id=1, source_target_pairs={{0,128},{4,160},{8,64},{12,96},{16,0},{20,32},{24,192},{28,224},{3... | collective-permute-start | bytes 589832 | tf_op jit(solution)/shard_map/ppermute | solution.py:265
  53.7 37.2 %all-to-all-start.2 = ((bf16[64,24,128]{2,1,0:T(8,128)(2,1)}), bf16[64,24,128]{2,1,0:T(8,128)(2,1)S(1)}, u32[]{:S(2)}, u32[]{:S(2)}) async-start(bf16[64,24,128]{2,1,0:T(8,128)(2,1)} %get-tuple-element.23), calls=%async_computation.2 | async-start | bytes 786432 | tf_op jit(solution)/shard_map/all_to_all | solution.py:217
  69.7 15.4 %collective-permute-start.10 = (bf16[32,768]{1,0:T(8,128)(2,1)S(1)}, bf16[32,768]{1,0:T(8,128)(2,1)S(1)}, u32[]{:S(2)}, u32[]{:S(2)}) collective-permute-start(bf16[32,768]{1,0:T(8,128)(2,1)S(1)} %bitcast.85), channel_id=1, source_target_pairs={{0,96},{32,128},{64,160},{96,192},{128,224},{160,0},{192,32},{224,... | collective-permute-start | bytes 147464 | tf_op jit(solution)/shard_map/ppermute | solution.py:204
  72.9 13.8 %collective-permute-start.11 = (bf16[32,768]{1,0:T(8,128)(2,1)S(1)}, bf16[32,768]{1,0:T(8,128)(2,1)S(1)}, u32[]{:S(2)}, u32[]{:S(2)}) collective-permute-start(bf16[32,768]{1,0:T(8,128)(2,1)S(1)} %bitcast.83), channel_id=1, source_target_pairs={{0,128},{32,160},{64,192},{96,224},{128,0},{160,32},{192,64},{224,... | collective-permute-start | bytes 147464 | tf_op jit(solution)/shard_map/ppermute | solution.py:204
  82.8 4.4 %collective-permute-start.12 = (bf16[32,768]{1,0:T(8,128)(2,1)S(1)}, bf16[32,768]{1,0:T(8,128)(2,1)S(1)}, u32[]{:S(2)}, u32[]{:S(2)}) collective-permute-start(bf16[32,768]{1,0:T(8,128)(2,1)S(1)} %bitcast.82), channel_id=1, source_target_pairs={{0,160},{32,192},{64,224},{96,0},{128,32},{160,64},{192,96},{224,1... | collective-permute-start | bytes 147464 | tf_op jit(solution)/shard_map/ppermute | solution.py:204
  82.9 4.6 %collective-permute-start.13 = (bf16[32,768]{1,0:T(8,128)(2,1)S(1)}, bf16[32,768]{1,0:T(8,128)(2,1)S(1)}, u32[]{:S(2)}, u32[]{:S(2)}) collective-permute-start(bf16[32,768]{1,0:T(8,128)(2,1)S(1)} %bitcast.84), channel_id=1, source_target_pairs={{0,192},{32,224},{64,0},{96,32},{128,64},{160,96},{192,128},{224,1... | collective-permute-start | bytes 147464 | tf_op jit(solution)/shard_map/ppermute | solution.py:204
  85.0 3.3 %collective-permute-start.14 = (bf16[32,768]{1,0:T(8,128)(2,1)S(1)}, bf16[32,768]{1,0:T(8,128)(2,1)S(1)}, u32[]{:S(2)}, u32[]{:S(2)}) collective-permute-start(bf16[32,768]{1,0:T(8,128)(2,1)S(1)} %bitcast.86), channel_id=1, source_target_pairs={{0,224},{32,0},{64,32},{96,64},{128,96},{160,128},{192,160},{224,1... | collective-permute-start | bytes 147464 | tf_op jit(solution)/shard_map/ppermute | solution.py:204
  85.1 5.1 %collective-permute-start.8 = (bf16[32,768]{1,0:T(8,128)(2,1)S(1)}, bf16[32,768]{1,0:T(8,128)(2,1)S(1)}, u32[]{:S(2)}, u32[]{:S(2)}) collective-permute-start(bf16[32,768]{1,0:T(8,128)(2,1)S(1)} %bitcast.88), channel_id=1, source_target_pairs={{0,32},{32,64},{64,96},{96,128},{128,160},{160,192},{192,224},{224... | collective-permute-start | bytes 147464 | tf_op jit(solution)/shard_map/ppermute | solution.py:204
  86.7 4.2 %collective-permute-start.9 = (bf16[32,768]{1,0:T(8,128)(2,1)S(1)}, bf16[32,768]{1,0:T(8,128)(2,1)S(1)}, u32[]{:S(2)}, u32[]{:S(2)}) collective-permute-start(bf16[32,768]{1,0:T(8,128)(2,1)S(1)} %bitcast.87), channel_id=1, source_target_pairs={{0,64},{32,96},{64,128},{96,160},{128,192},{160,224},{192,0},{224,... | collective-permute-start | bytes 147464 | tf_op jit(solution)/shard_map/ppermute | solution.py:204
  91.7 11.4 %all-to-all-start.3 = ((bf16[8,32,768]{2,1,0:T(8,128)(2,1)}), bf16[8,32,768]{2,1,0:T(8,128)(2,1)S(1)}, u32[]{:S(2)}, u32[]{:S(2)}) async-start(bf16[8,32,768]{2,1,0:T(8,128)(2,1)} %broadcast_in_dim.4), calls=%async_computation.3 | async-start | bytes 786432 | tf_op jit(solution)/shard_map/all_to_all | solution.py:217
  95.2 4.4 %collective-permute-start.4 = (f32[24,128]{1,0:T(8,128)S(1)}, f32[24,128]{1,0:T(8,128)S(1)}, u32[]{:S(2)}, u32[]{:S(2)}) collective-permute-start(f32[24,128]{1,0:T(8,128)S(1)} %convert_reduce_fusion), channel_id=1, source_target_pairs={{0,2},{1,3},{2,0},{3,1},{4,6},{5,7},{6,4},{7,5},{8,10},{9,11},{10,... | collective-permute-start | bytes 36872 | tf_op jit(solution)/shard_map/ppermute | solution.py:204
  95.8 4.1 %collective-permute-start.5 = (f32[24,128]{1,0:T(8,128)S(1)}, f32[24,128]{1,0:T(8,128)S(1)}, u32[]{:S(2)}, u32[]{:S(2)}) collective-permute-start(f32[24,128]{1,0:T(8,128)S(1)} %convert_reduce_fusion), channel_id=1, source_target_pairs={{0,1},{1,2},{2,3},{3,0},{4,5},{5,6},{6,7},{7,4},{8,9},{9,10},{10,1... | collective-permute-start | bytes 36872 | tf_op jit(solution)/shard_map/ppermute | solution.py:204
  97.1 2.8 %collective-permute-start.6 = (f32[24,128]{1,0:T(8,128)S(1)}, f32[24,128]{1,0:T(8,128)S(1)}, u32[]{:S(2)}, u32[]{:S(2)}) collective-permute-start(f32[24,128]{1,0:T(8,128)S(1)} %convert_reduce_fusion), channel_id=1, source_target_pairs={{0,3},{1,0},{2,1},{3,2},{4,7},{5,4},{6,5},{7,6},{8,11},{9,8},{10,9... | collective-permute-start | bytes 36872 | tf_op jit(solution)/shard_map/ppermute | solution.py:204
  103.8 20.5 %all-to-all-start.4 = ((bf16[64,16,128]{2,1,0:T(8,128)(2,1)}), bf16[64,16,128]{2,1,0:T(8,128)(2,1)S(1)}, u32[]{:S(2)}, u32[]{:S(2)}) async-start(bf16[64,16,128]{2,1,0:T(8,128)(2,1)} %broadcast_in_dim.5), calls=%async_computation.4 | async-start | bytes 524288 | tf_op jit(solution)/shard_map/all_to_all | solution.py:217
  112.4 1.6 %copy-start.1 = (bf16[32,96,256]{2,1,0:T(8,128)(2,1)S(1)}, bf16[32,96,256]{2,1,0:T(8,128)(2,1)}, u32[]{:S(2)}) copy-start(bf16[32,96,256]{2,1,0:T(8,128)(2,1)} %align_ref.3) | copy-start | bytes 4718596
  112.4 1.6 %copy-start.4 = (bf16[256,64]{0,1:T(8,128)(2,1)S(1)}, bf16[256,64]{0,1:T(8,128)(2,1)}, u32[]{:S(2)}) copy-start(bf16[256,64]{0,1:T(8,128)(2,1)} %param.6) | copy-start | bytes 98308

commit v4 on v3

--- a/solution.py
+++ b/solution.py
@@ -246,8 +246,7 @@
         start = depth_count - 1 - depth_idx
         return lax.dynamic_slice_in_dim(jnp.concatenate([chunks, chunks]), start, depth_count, 0)
 
-    right_turned = turned_back(right).reshape(seq_count, quarter * latent)
-    right = right.reshape(seq_count, quarter * latent)
+    right = turned_back(right).reshape(seq_count, quarter * latent)
 
     adj = jnp.transpose(adjoint_incoming, (1, 0, 2))
     adj, left_mine = lax.optimization_barrier((adj, left_mine))
@@ -255,20 +254,25 @@
     grad_outer, grad_left = grad_outer_of(adj, final_matrix, right, 1.0 / seq_count)
     grad_right = lax.dot_general(left, grad_outer, (((1,), (0,)), ((), ())), preferred_element_type=F32)
     grad_right = (grad_right / seq_count).astype(BF)
-    grad_left = grad_left.reshape(depth_count, share, latent * amino)
-    grads = exchange(jnp.concatenate([grad_left, turned_back(grad_right)], axis=-1), "depth")
-    pair_t, weight = outer_of(left, right_turned, adj, final_matrix, final_offset, 1.0 / seq_count, plane_count)
+    grads = jnp.concatenate([grad_left, grad_right], axis=-1).reshape(depth_count, share, -1)
+    grads = [grads[0]] + [shifted(grads[k], "depth", -k) for k in range(1, depth_count)]
+    pair_t, weight = outer_of(left, right, adj, final_matrix, final_offset, 1.0 / seq_count, plane_count)
     contact_delta = jnp.transpose(pair_t, (1, 0, 2))
 
-    left_sum = jnp.sum(grads[..., : latent * amino].astype(F32), axis=0).astype(BF)
+    left_sum = sum(g[:, : latent * amino].astype(F32) for g in grads).astype(BF)
     weight, left_sum = lax.optimization_barrier((weight, left_sum))
     left_part = lax.ppermute(left_sum, PLANE, back)
     piece = latent * amino // row_count
     left_pieces = left_part.reshape(share, row_count, piece).transpose(1, 0, 2)
-    right_pieces = grads[..., latent * amino :].reshape(depth_count, share, row_count // depth_count, piece)
-    right_pieces = right_pieces.transpose(0, 2, 1, 3).reshape(row_count, share, piece)
-    pieces = jnp.concatenate([left_pieces, right_pieces], axis=-1)
-    turned = lax.dynamic_slice_in_dim(jnp.concatenate([pieces, pieces]), lax.axis_index("row"), row_count, 0)
+    row_idx = lax.axis_index("row")
+    right_pieces = jnp.concatenate([g[:, latent * amino :] for g in grads] * 2, axis=-1)
+    right_start = (row_idx - depth_idx * (row_count // depth_count)) % row_count
+    right_turned = lax.dynamic_slice_in_dim(right_pieces, right_start * piece, row_count * piece, 1)
+    left_turned = lax.dynamic_slice_in_dim(jnp.concatenate([left_pieces, left_pieces]), row_idx, row_count, 0)
+    turned = [
+        jnp.concatenate([left_turned[k], right_turned[:, k * piece : (k + 1) * piece]], axis=-1)
+        for k in range(row_count)
+    ]
     reduced = turned[0].astype(F32)
     for k in range(1, row_count):
         reduced = reduced + shifted(turned[k], "row", k).astype(F32)

time: 126 us -> 129 us (1.024)
  local copies, waits for them, and re-layouts: 9.61 us -> 15.6 us
  waiting for transfers between devices: 21.4 us -> 15.6 us
  starting transfers between devices: 67.9 us -> 72.6 us
    ppermute x1, starting transfers between devices: 1.2 us -> 9.17 us  [step(): left_part = lax.ppermute(left_sum, PLANE, back)]
    all_to_all x5 -> x4, waiting for transfers between devices: 14.2 us -> 8.5 us  [exchange(): return lax.all_to_all(pieces, axis, split_axis=0, concat_axis=0, tiled=True)]
    ppermute x13 -> x16, starting transfers between devices: 25.8 us -> 20.9 us  [shifted(): return lax.ppermute(value, axis, [(q, (q + by) % n) for q in range(n)])]
    unnamed x27 -> x32, local copies, waits for them, and re-layouts: 3.44 us -> 8.17 us
    ppermute x13 -> x16, waiting for transfers between devices: 7.19 us -> 4.73 us  [shifted(): return lax.ppermute(value, axis, [(q, (q + by) % n) for q in range(n)])]
    ppermute x1, waiting for transfers between devices: 0.01 us -> 2.39 us  [step(): lax.ppermute(left_own.reshape(share, latent * amino), PLANE, there)]
    all_to_all x5 -> x4, starting transfers between devices: 32.9 us -> 35.1 us  [exchange(): return lax.all_to_all(pieces, axis, split_axis=0, concat_axis=0, tiled=True)]
    concatenate x0 -> x1, local copies, waits for them, and re-layouts: none -> 1.42 us  [step(): jnp.concatenate([g[:, latent * amino:] for g in grads] * 2, axis=-1)]
  transfers between devices with their start and end apart: 20 -> 22, of which waited for: 11 -> 9; matrix products, arithmetic and copies ran while one was open for 5% -> 9% of each run, Pallas kernels for 14% -> 13%
where the time goes in v4:
time: 129 us; the launch traced here: 128 us
  starting transfers between devices  72.6 us (56%)
  Pallas kernels  19.3 us (15%)
  local copies, waits for them, and re-layouts  15.6 us (12%)
  waiting for transfers between devices  15.6 us (12%)
  other arithmetic  3.35 us (3%)
    all_to_all x4, starting transfers between devices, exchange(): return lax.all_to_all(pieces, axis, split_axis=0, concat_axis=0, tiled=True)  35.1 us
    ppermute x16, starting transfers between devices, shifted(): return lax.ppermute(value, axis, [(q, (q + by) % n) for q in range(n)])  20.9 us
    ppermute x1, starting transfers between devices, step(): left_part = lax.ppermute(left_sum, PLANE, back)  9.17 us
    all_to_all x4, waiting for transfers between devices, exchange(): return lax.all_to_all(pieces, axis, split_axis=0, concat_axis=0, tiled=True)  8.5 us
    unnamed x32, local copies, waits for them, and re-layouts  8.17 us
    ppermute x1, starting transfers between devices, step(): lax.ppermute(left_own.reshape(share, latent * amino), PLANE, there)  7.39 us
    pallas_call x1, Pallas kernels, outer_of(): pl.pallas_call(lambda *refs: outer_kernel(scale, *refs), grid=(left.shape...  6.93 us
    pallas_call x1, Pallas kernels, grad_outer_of(): pl.pallas_call(lambda *refs: grad_outer_kernel(scale, *refs), grid=(group...  5.81 us
  transfers between devices with their start and end apart: 22, of which 9 were waited for; matrix products, arithmetic and copies ran while one was open for 9% of the time, Pallas kernels for 13%

profile of v4, /device:TPU:1, one launch (start us, length us, event | category | flops | bytes accessed | tf_op | source)
XLA Modules:
  0.0 128.3 jit_solution(15447377084761199729)
XLA Ops:
  0.6 1.4 %copy-done = bf16[32,96,256]{2,1,0:T(8,128)(2,1)S(1)} copy-done((bf16[32,96,256]{2,1,0:T(8,128)(2,1)S(1)}, bf16[32,96,256]{2,1,0:T(8,128)(2,1)}, u32[]{:S(2)}) %copy-start) | copy-done | bytes 1572888
  2.0 0.8 copy-done.4
  2.8 2.6 %panels.1 = (bf16[32,32,96]{2,1,0:T(8,128)(2,1)S(1)}, bf16[32,96,32]{2,1,0:T(8,128)(2,1)S(1)}) custom-call(bf16[32,96,256]{2,1,0:T(8,128)(2,1)S(1)} %copy-done, bf16[64,256]{1,0:T(8,128)(2,1)S(1)} %bitcast.49), custom_call_target="tpu_custom_call" | custom-call | tf_op jit(solution)/shard_map/panels/pallas_call | solution.py:43
  5.9 0.7 copy.20
  6.6 5.0 %all-to-all-start = ((bf16[4,32,768]{2,1,0:T(8,128)(2,1)}), bf16[4,32,768]{2,1,0:T(8,128)(2,1)S(1)}, u32[]{:S(2)}, u32[]{:S(2)}) async-start(bf16[4,32,768]{2,1,0:T(8,128)(2,1)} %copy.20), calls=%async_computation | async-start | bytes 393216 | tf_op jit(solution)/shard_map/all_to_all | solution.py:217
  11.9 7.4 %collective-permute-start = (bf16[32,3072]{1,0:T(8,128)(2,1)S(1)}, bf16[32,3072]{1,0:T(8,128)(2,1)S(1)}, u32[]{:S(2)}, u32[]{:S(2)}) collective-permute-start(bf16[32,3072]{1,0:T(8,128)(2,1)S(1)} %reshape.49), channel_id=1, source_target_pairs={{128,0},{160,4},{64,8},{96,12},{0,16},{32,20},{192,24},{224,28},{1... | collective-permute-start | bytes 589832 | tf_op jit(solution)/shard_map/ppermute | solution.py:240
  19.3 1.1 copy.29
  20.6 2.4 %collective-permute-done = bf16[32,3072]{1,0:T(8,128)(2,1)S(1)} collective-permute-done((bf16[32,3072]{1,0:T(8,128)(2,1)S(1)}, bf16[32,3072]{1,0:T(8,128)(2,1)S(1)}, u32[]{:S(2)}, u32[]{:S(2)}) %collective-permute-start) | collective-permute-done | bytes 196640 | tf_op jit(solution)/shard_map/ppermute | solution.py:240
  23.0 1.5 %collective-permute-start.1 = (bf16[32,3072]{1,0:T(8,128)(2,1)S(1)}, bf16[32,3072]{1,0:T(8,128)(2,1)S(1)}, u32[]{:S(2)}, u32[]{:S(2)}) collective-permute-start(bf16[32,3072]{1,0:T(8,128)(2,1)S(1)} %collective-permute-done), channel_id=1, source_target_pairs={{0,1},{1,2},{2,3},{3,0},{4,5},{5,6},{6,7},{7,4},{8,9},{9,10},{10,1... | collective-permute-start | bytes 589832 | tf_op jit(solution)/shard_map/ppermute | solution.py:204
  24.5 2.4 %collective-permute-start.2 = (bf16[32,3072]{1,0:T(8,128)(2,1)S(1)}, bf16[32,3072]{1,0:T(8,128)(2,1)S(1)}, u32[]{:S(2)}, u32[]{:S(2)}) collective-permute-start(bf16[32,3072]{1,0:T(8,128)(2,1)S(1)} %collective-permute-done), channel_id=1, source_target_pairs={{0,2},{1,3},{2,0},{3,1},{4,6},{5,7},{6,4},{7,5},{8,10},{9,11},{10,... | collective-permute-start | bytes 589832 | tf_op jit(solution)/shard_map/ppermute | solution.py:204
  26.9 1.2 collective-permute-start.3
  28.1 5.8 %grad_outer.1 = (bf16[3072,768]{1,0:T(8,128)(2,1)S(1)}, bf16[128,3072]{1,0:T(8,128)(2,1)S(1)}) custom-call(bf16[24,96,128]{2,1,0:T(8,128)(2,1)S(1)} %bitcast.43, bf16[1024,128]{1,0:T(8,128)(2,1)S(1)} %copy-done.2, bf16[128,768]{1,0:T(8,128)(2,1)S(1)} %bitcast.45), custom_call_target="tpu_custom_call" | custom-call | tf_op jit(solution)/shard_map/grad_outer/pallas_call | solution.py:126
  34.1 0.8 fusion
  34.9 0.9 pad_maximum_fusion.2
  35.7 0.6 collective-permute-start.4
  36.3 1.5 %collective-permute-start.5 = (bf16[32,3840]{1,0:T(8,128)(2,1)}, bf16[32,3840]{1,0:T(8,128)(2,1)S(1)}, u32[]{:S(2)}, u32[]{:S(2)}) collective-permute-start(bf16[32,3840]{1,0:T(8,128)(2,1)} %get-tuple-element.41), channel_id=1, source_target_pairs={{0,2},{1,3},{2,0},{3,1},{4,6},{5,7},{6,4},{7,5},{8,10},{9,11},{10,... | collective-permute-start | bytes 737288 | tf_op jit(solution)/shard_map/ppermute | solution.py:204
  37.8 6.9 %outer.1 = (bf16[24,96,128]{2,1,0:T(8,128)(2,1)S(1)}, bf16[64,24,128]{2,1,0:T(8,128)(2,1)S(1)}) custom-call(bf16[128,3072]{1,0:T(8,128)(2,1)S(1)} %constant_dynamic-update-slice_fusion.refs_0_, bf16[128,768]{1,0:T(8,128)(2,1)S(1)} %bitcast.46, bf16[24,96,128]{2,1,0:T(8,128)(2,1)S(1)} %bitcast.44, bf16[1024,128]{1,0:T(8,128)(2,1)S(1)} %copy-done.2, ...), custom_call_target="tpu_custom_call" | custom-call | tf_op jit(solution)/shard_map/outer/pallas_call | solution.py:184
  44.8 0.9 slice_dynamic-update-slice_fusion.4
  45.7 0.7 collective-permute-done.6
  46.4 1.2 add_convert_fusion
  47.7 9.2 %collective-permute-start.10 = (bf16[32,3072]{1,0:T(8,128)(2,1)S(1)}, bf16[32,3072]{1,0:T(8,128)(2,1)S(1)}, u32[]{:S(2)}, u32[]{:S(2)}) collective-permute-start(bf16[32,3072]{1,0:T(8,128)(2,1)S(1)} %add_convert_fusion), channel_id=1, source_target_pairs={{0,128},{4,160},{8,64},{12,96},{16,0},{20,32},{24,192},{28,224},{3... | collective-permute-start | bytes 589832 | tf_op jit(solution)/shard_map/ppermute | solution.py:264
  56.9 14.0 %all-to-all-start.1 = ((bf16[64,24,128]{2,1,0:T(8,128)(2,1)}), bf16[64,24,128]{2,1,0:T(8,128)(2,1)S(1)}, u32[]{:S(2)}, u32[]{:S(2)}) async-start(bf16[64,24,128]{2,1,0:T(8,128)(2,1)} %copy-done.3), calls=%async_computation.1 | async-start | bytes 786432 | tf_op jit(solution)/shard_map/all_to_all | solution.py:217
  70.9 1.4 %slice_dynamic-update-slice_fusion.5 = bf16[32,6144]{1,0:T(8,128)(2,1)} fusion(bf16[32,6144]{1,0:T(8,128)(2,1)} %copy-done.9, bf16[32,3840]{1,0:T(8,128)(2,1)} %collective-permute-done.4), kind=kLoop, calls=%fused_computation.29 | loop fusion | bytes 98304
  72.3 1.4 %slice_dynamic-update-slice_fusion.3 = bf16[32,6144]{1,0:T(8,128)(2,1)} fusion(bf16[32,6144]{1,0:T(8,128)(2,1)} %slice_dynamic-update-slice_fusion.5, bf16[32,3840]{1,0:T(8,128)(2,1)} %copy-done.7), kind=kLoop, calls=%fused_computation.27 | loop fusion | bytes 98304
  73.7 1.4 %slice_dynamic-update-slice_fusion.1 = bf16[32,6144]{1,0:T(8,128)(2,1)} fusion(bf16[32,6144]{1,0:T(8,128)(2,1)} %slice_dynamic-update-slice_fusion.3, bf16[32,3840]{1,0:T(8,128)(2,1)} %copy-done.8), kind=kLoop, calls=%fused_computation.25 | loop fusion | bytes 98304 | tf_op jit(solution)/shard_map/concatenate | solution.py:268
  75.1 0.9 constant_dynamic-slice_fusion.4
  76.2 1.4 %collective-permute-start.11 = (bf16[32,768]{1,0:T(8,128)(2,1)S(1)}, bf16[32,768]{1,0:T(8,128)(2,1)S(1)}, u32[]{:S(2)}, u32[]{:S(2)}) collective-permute-start(bf16[32,768]{1,0:T(8,128)(2,1)S(1)} %pad_maximum_fusion.3), channel_id=1, source_target_pairs={{0,32},{32,64},{64,96},{96,128},{128,160},{160,192},{192,224},{224... | collective-permute-start | bytes 147464 | tf_op jit(solution)/shard_map/ppermute | solution.py:204
  77.7 1.2 collective-permute-start.12
  78.9 2.0 %collective-permute-start.13 = (bf16[32,768]{1,0:T(8,128)(2,1)S(1)}, bf16[32,768]{1,0:T(8,128)(2,1)S(1)}, u32[]{:S(2)}, u32[]{:S(2)}) collective-permute-start(bf16[32,768]{1,0:T(8,128)(2,1)S(1)} %pad_maximum_fusion.5), channel_id=1, source_target_pairs={{0,96},{32,128},{64,160},{96,192},{128,224},{160,0},{192,32},{224,... | collective-permute-start | bytes 147464 | tf_op jit(solution)/shard_map/ppermute | solution.py:204
  80.9 1.6 %collective-permute-start.14 = (bf16[32,768]{1,0:T(8,128)(2,1)S(1)}, bf16[32,768]{1,0:T(8,128)(2,1)S(1)}, u32[]{:S(2)}, u32[]{:S(2)}) collective-permute-start(bf16[32,768]{1,0:T(8,128)(2,1)S(1)} %pad_maximum_fusion.6), channel_id=1, source_target_pairs={{0,128},{32,160},{64,192},{96,224},{128,0},{160,32},{192,64},{224,... | collective-permute-start | bytes 147464 | tf_op jit(solution)/shard_map/ppermute | solution.py:204
  82.4 2.9 %collective-permute-start.15 = (bf16[32,768]{1,0:T(8,128)(2,1)S(1)}, bf16[32,768]{1,0:T(8,128)(2,1)S(1)}, u32[]{:S(2)}, u32[]{:S(2)}) collective-permute-start(bf16[32,768]{1,0:T(8,128)(2,1)S(1)} %pad_maximum_fusion.7), channel_id=1, source_target_pairs={{0,160},{32,192},{64,224},{96,0},{128,32},{160,64},{192,96},{224,1... | collective-permute-start | bytes 147464 | tf_op jit(solution)/shard_map/ppermute | solution.py:204
  85.4 1.2 collective-permute-start.16
  86.6 1.3 collective-permute-done.14
  87.9 0.9 collective-permute-done.16
  88.8 0.7 collective-permute-done.17
  89.6 0.8 broadcast_in_dim.4
  90.4 3.8 %all-to-all-start.2 = ((bf16[8,32,768]{2,1,0:T(8,128)(2,1)}), bf16[8,32,768]{2,1,0:T(8,128)(2,1)S(1)}, u32[]{:S(2)}, u32[]{:S(2)}) async-start(bf16[8,32,768]{2,1,0:T(8,128)(2,1)} %broadcast_in_dim.4), calls=%async_computation.2 | async-start | bytes 786432 | tf_op jit(solution)/shard_map/all_to_all | solution.py:217
  94.3 0.8 collective-permute-start.7
  95.6 2.1 %collective-permute-start.9 = (f32[24,128]{1,0:T(8,128)S(1)}, f32[24,128]{1,0:T(8,128)S(1)}, u32[]{:S(2)}, u32[]{:S(2)}) collective-permute-start(f32[24,128]{1,0:T(8,128)S(1)} %convert_reduce_fusion), channel_id=1, source_target_pairs={{0,3},{1,0},{2,1},{3,2},{4,7},{5,4},{6,5},{7,6},{8,11},{9,8},{10,9... | collective-permute-start | bytes 36872 | tf_op jit(solution)/shard_map/ppermute | solution.py:204
  97.8 0.7 collective-permute-done.7
  98.9 2.2 %all-to-all-done.2 = bf16[8,32,768]{2,1,0:T(8,128)(2,1)S(1)} async-done(((bf16[8,32,768]{2,1,0:T(8,128)(2,1)}), bf16[8,32,768]{2,1,0:T(8,128)(2,1)S(1)}, u32[]{:S(2)}, u32[]{:S(2)}) %all-to-all-start.2) | async-done | bytes 393248 | tf_op jit(solution)/shard_map/all_to_all | solution.py:217
  101.0 0.7 broadcast_in_dim.5
  101.8 12.3 %all-to-all-start.3 = ((bf16[64,16,128]{2,1,0:T(8,128)(2,1)}), bf16[64,16,128]{2,1,0:T(8,128)(2,1)S(1)}, u32[]{:S(2)}, u32[]{:S(2)}) async-start(bf16[64,16,128]{2,1,0:T(8,128)(2,1)} %broadcast_in_dim.5), calls=%async_computation.3 | async-start | bytes 524288 | tf_op jit(solution)/shard_map/all_to_all | solution.py:217
  114.0 1.0 copy.25
  115.6 0.8 reshape.56
  117.3 3.9 %align.1 = f32[32,96,256]{2,1,0:T(8,128)} custom-call(bf16[32,96,256]{2,1,0:T(8,128)(2,1)S(1)} %copy-done.1, bf16[32,32,96]{2,1,0:T(8,128)(2,1)S(1)} %bitcast.47, bf16[32,96,32]{2,1,0:T(8,128)(2,1)S(1)} %copy.24.right_ref, bf16[64,256]{1,0:T(8,128)(2,1)S(1)} %bitcast.50), custom_call_target="tpu_custom_call" | custom-call | tf_op jit(solution)/shard_map/align/pallas_call | solution.py:76
  121.1 6.3 %all-to-all-done.3 = bf16[64,16,128]{2,1,0:T(8,128)(2,1)S(1)} async-done(((bf16[64,16,128]{2,1,0:T(8,128)(2,1)}), bf16[64,16,128]{2,1,0:T(8,128)(2,1)S(1)}, u32[]{:S(2)}, u32[]{:S(2)}) %all-to-all-start.3) | async-done | bytes 262176 | tf_op jit(solution)/shard_map/all_to_all | solution.py:217
  127.5 0.8 bitcast_convert_fusion
  (67 shorter events, 3.7 us)
Async XLA Ops:
  0.6 1.4 %copy-start = (bf16[32,96,256]{2,1,0:T(8,128)(2,1)S(1)}, bf16[32,96,256]{2,1,0:T(8,128)(2,1)}, u32[]{:S(2)}) copy-start(bf16[32,96,256]{2,1,0:T(8,128)(2,1)} %align_ref.3) | copy-start | bytes 4718596
  2.0 0.8 copy-start.4
  2.8 25.3 %copy-start.2 = (bf16[1024,128]{1,0:T(8,128)(2,1)S(1)}, bf16[1024,128]{1,0:T(8,128)(2,1)}, u32[]{:S(2)}) copy-start(bf16[1024,128]{1,0:T(8,128)(2,1)} %refs_1_.1) | copy-start | bytes 786436
  6.6 13.9 %all-to-all-start = ((bf16[4,32,768]{2,1,0:T(8,128)(2,1)}), bf16[4,32,768]{2,1,0:T(8,128)(2,1)S(1)}, u32[]{:S(2)}, u32[]{:S(2)}) async-start(bf16[4,32,768]{2,1,0:T(8,128)(2,1)} %copy.20), calls=%async_computation | async-start | bytes 393216 | tf_op jit(solution)/shard_map/all_to_all | solution.py:217
  11.9 11.1 %collective-permute-start = (bf16[32,3072]{1,0:T(8,128)(2,1)S(1)}, bf16[32,3072]{1,0:T(8,128)(2,1)S(1)}, u32[]{:S(2)}, u32[]{:S(2)}) collective-permute-start(bf16[32,3072]{1,0:T(8,128)(2,1)S(1)} %reshape.49), channel_id=1, source_target_pairs={{128,0},{160,4},{64,8},{96,12},{0,16},{32,20},{192,24},{224,28},{1... | collective-permute-start | bytes 589832 | tf_op jit(solution)/shard_map/ppermute | solution.py:240
  23.0 11.0 %collective-permute-start.1 = (bf16[32,3072]{1,0:T(8,128)(2,1)S(1)}, bf16[32,3072]{1,0:T(8,128)(2,1)S(1)}, u32[]{:S(2)}, u32[]{:S(2)}) collective-permute-start(bf16[32,3072]{1,0:T(8,128)(2,1)S(1)} %collective-permute-done), channel_id=1, source_target_pairs={{0,1},{1,2},{2,3},{3,0},{4,5},{5,6},{6,7},{7,4},{8,9},{9,10},{10,1... | collective-permute-start | bytes 589832 | tf_op jit(solution)/shard_map/ppermute | solution.py:204
  24.5 9.5 %collective-permute-start.2 = (bf16[32,3072]{1,0:T(8,128)(2,1)S(1)}, bf16[32,3072]{1,0:T(8,128)(2,1)S(1)}, u32[]{:S(2)}, u32[]{:S(2)}) collective-permute-start(bf16[32,3072]{1,0:T(8,128)(2,1)S(1)} %collective-permute-done), channel_id=1, source_target_pairs={{0,2},{1,3},{2,0},{3,1},{4,6},{5,7},{6,4},{7,5},{8,10},{9,11},{10,... | collective-permute-start | bytes 589832 | tf_op jit(solution)/shard_map/ppermute | solution.py:204
  26.9 7.1 %collective-permute-start.3 = (bf16[32,3072]{1,0:T(8,128)(2,1)S(1)}, bf16[32,3072]{1,0:T(8,128)(2,1)S(1)}, u32[]{:S(2)}, u32[]{:S(2)}) collective-permute-start(bf16[32,3072]{1,0:T(8,128)(2,1)S(1)} %collective-permute-done), channel_id=1, source_target_pairs={{0,3},{1,0},{2,1},{3,2},{4,7},{5,4},{6,5},{7,6},{8,11},{9,8},{10,9... | collective-permute-start | bytes 589832 | tf_op jit(solution)/shard_map/ppermute | solution.py:204
  33.9 3.9 %copy-start.6 = (f32[128]{0:T(128)S(1)}, f32[128]{0:T(128)}, u32[]{:S(2)}) copy-start(f32[128]{0:T(128)} %param.8) | copy-start | bytes 1540
  35.7 9.0 %collective-permute-start.4 = (bf16[32,3840]{1,0:T(8,128)(2,1)}, bf16[32,3840]{1,0:T(8,128)(2,1)}, u32[]{:S(2)}, u32[]{:S(2)}) collective-permute-start(bf16[32,3840]{1,0:T(8,128)(2,1)} %get-tuple-element.40), channel_id=1, source_target_pairs={{0,3},{1,0},{2,1},{3,2},{4,7},{5,4},{6,5},{7,6},{8,11},{9,8},{10,9... | collective-permute-start | bytes 737288 | tf_op jit(solution)/shard_map/ppermute | solution.py:204
  36.3 9.3 %collective-permute-start.5 = (bf16[32,3840]{1,0:T(8,128)(2,1)}, bf16[32,3840]{1,0:T(8,128)(2,1)S(1)}, u32[]{:S(2)}, u32[]{:S(2)}) collective-permute-start(bf16[32,3840]{1,0:T(8,128)(2,1)} %get-tuple-element.41), channel_id=1, source_target_pairs={{0,2},{1,3},{2,0},{3,1},{4,6},{5,7},{6,4},{7,5},{8,10},{9,11},{10,... | collective-permute-start | bytes 737288 | tf_op jit(solution)/shard_map/ppermute | solution.py:204
  37.8 8.6 %collective-permute-start.6 = (bf16[32,3840]{1,0:T(8,128)(2,1)}, bf16[32,3840]{1,0:T(8,128)(2,1)S(1)}, u32[]{:S(2)}, u32[]{:S(2)}) collective-permute-start(bf16[32,3840]{1,0:T(8,128)(2,1)} %get-tuple-element.42), channel_id=1, source_target_pairs={{0,1},{1,2},{2,3},{3,0},{4,5},{5,6},{6,7},{7,4},{8,9},{9,10},{10,1... | collective-permute-start | bytes 737288 | tf_op jit(solution)/shard_map/ppermute | solution.py:204
  44.7 2.9 %copy-start.3 = (bf16[64,24,128]{2,1,0:T(8,128)(2,1)}, bf16[64,24,128]{2,1,0:T(8,128)(2,1)S(1)}, u32[]{:S(2)}) copy-start(bf16[64,24,128]{2,1,0:T(8,128)(2,1)S(1)} %get-tuple-element.23) | copy-start | bytes 1179652
  45.6 2.0 %copy-start.7 = (bf16[32,3840]{1,0:T(8,128)(2,1)}, bf16[32,3840]{1,0:T(8,128)(2,1)S(1)}, u32[]{:S(2)}) copy-start(bf16[32,3840]{1,0:T(8,128)(2,1)S(1)} %collective-permute-done.5) | copy-start | bytes 737284
  46.4 1.3 %copy-start.8 = (bf16[32,3840]{1,0:T(8,128)(2,1)}, bf16[32,3840]{1,0:T(8,128)(2,1)S(1)}, u32[]{:S(2)}) copy-start(bf16[32,3840]{1,0:T(8,128)(2,1)S(1)} %collective-permute-done.6) | copy-start | bytes 737284
  46.4 1.3 %copy-start.9 = (bf16[32,6144]{1,0:T(8,128)(2,1)}, bf16[32,6144]{1,0:T(8,128)(2,1)S(1)}, u32[]{:S(2)}) copy-start(bf16[32,6144]{1,0:T(8,128)(2,1)S(1)} %slice_dynamic-update-slice_fusion.7) | copy-start | bytes 1179652
  47.7 28.4 %collective-permute-start.10 = (bf16[32,3072]{1,0:T(8,128)(2,1)S(1)}, bf16[32,3072]{1,0:T(8,128)(2,1)S(1)}, u32[]{:S(2)}, u32[]{:S(2)}) collective-permute-start(bf16[32,3072]{1,0:T(8,128)(2,1)S(1)} %add_convert_fusion), channel_id=1, source_target_pairs={{0,128},{4,160},{8,64},{12,96},{16,0},{20,32},{24,192},{28,224},{3... | collective-permute-start | bytes 589832 | tf_op jit(solution)/shard_map/ppermute | solution.py:264
  56.9 32.7 %all-to-all-start.1 = ((bf16[64,24,128]{2,1,0:T(8,128)(2,1)}), bf16[64,24,128]{2,1,0:T(8,128)(2,1)S(1)}, u32[]{:S(2)}, u32[]{:S(2)}) async-start(bf16[64,24,128]{2,1,0:T(8,128)(2,1)} %copy-done.3), calls=%async_computation.1 | async-start | bytes 786432 | tf_op jit(solution)/shard_map/all_to_all | solution.py:217
  76.2 9.2 %collective-permute-start.11 = (bf16[32,768]{1,0:T(8,128)(2,1)S(1)}, bf16[32,768]{1,0:T(8,128)(2,1)S(1)}, u32[]{:S(2)}, u32[]{:S(2)}) collective-permute-start(bf16[32,768]{1,0:T(8,128)(2,1)S(1)} %pad_maximum_fusion.3), channel_id=1, source_target_pairs={{0,32},{32,64},{64,96},{96,128},{128,160},{160,192},{192,224},{224... | collective-permute-start | bytes 147464 | tf_op jit(solution)/shard_map/ppermute | solution.py:204
  77.7 8.9 %collective-permute-start.12 = (bf16[32,768]{1,0:T(8,128)(2,1)S(1)}, bf16[32,768]{1,0:T(8,128)(2,1)S(1)}, u32[]{:S(2)}, u32[]{:S(2)}) collective-permute-start(bf16[32,768]{1,0:T(8,128)(2,1)S(1)} %pad_maximum_fusion.4), channel_id=1, source_target_pairs={{0,64},{32,96},{64,128},{96,160},{128,192},{160,224},{192,0},{224,... | collective-permute-start | bytes 147464 | tf_op jit(solution)/shard_map/ppermute | solution.py:204
  78.9 7.7 %collective-permute-start.13 = (bf16[32,768]{1,0:T(8,128)(2,1)S(1)}, bf16[32,768]{1,0:T(8,128)(2,1)S(1)}, u32[]{:S(2)}, u32[]{:S(2)}) collective-permute-start(bf16[32,768]{1,0:T(8,128)(2,1)S(1)} %pad_maximum_fusion.5), channel_id=1, source_target_pairs={{0,96},{32,128},{64,160},{96,192},{128,224},{160,0},{192,32},{224,... | collective-permute-start | bytes 147464 | tf_op jit(solution)/shard_map/ppermute | solution.py:204
  80.9 7.0 %collective-permute-start.14 = (bf16[32,768]{1,0:T(8,128)(2,1)S(1)}, bf16[32,768]{1,0:T(8,128)(2,1)S(1)}, u32[]{:S(2)}, u32[]{:S(2)}) collective-permute-start(bf16[32,768]{1,0:T(8,128)(2,1)S(1)} %pad_maximum_fusion.6), channel_id=1, source_target_pairs={{0,128},{32,160},{64,192},{96,224},{128,0},{160,32},{192,64},{224,... | collective-permute-start | bytes 147464 | tf_op jit(solution)/shard_map/ppermute | solution.py:204
  82.4 5.4 %collective-permute-start.15 = (bf16[32,768]{1,0:T(8,128)(2,1)S(1)}, bf16[32,768]{1,0:T(8,128)(2,1)S(1)}, u32[]{:S(2)}, u32[]{:S(2)}) collective-permute-start(bf16[32,768]{1,0:T(8,128)(2,1)S(1)} %pad_maximum_fusion.7), channel_id=1, source_target_pairs={{0,160},{32,192},{64,224},{96,0},{128,32},{160,64},{192,96},{224,1... | collective-permute-start | bytes 147464 | tf_op jit(solution)/shard_map/ppermute | solution.py:204
  85.4 3.4 %collective-permute-start.16 = (bf16[32,768]{1,0:T(8,128)(2,1)S(1)}, bf16[32,768]{1,0:T(8,128)(2,1)S(1)}, u32[]{:S(2)}, u32[]{:S(2)}) collective-permute-start(bf16[32,768]{1,0:T(8,128)(2,1)S(1)} %pad_maximum_fusion.8), channel_id=1, source_target_pairs={{0,192},{32,224},{64,0},{96,32},{128,64},{160,96},{192,128},{224,1... | collective-permute-start | bytes 147464 | tf_op jit(solution)/shard_map/ppermute | solution.py:204
  86.6 2.9 %collective-permute-start.17 = (bf16[32,768]{1,0:T(8,128)(2,1)S(1)}, bf16[32,768]{1,0:T(8,128)(2,1)S(1)}, u32[]{:S(2)}, u32[]{:S(2)}) collective-permute-start(bf16[32,768]{1,0:T(8,128)(2,1)S(1)} %pad_maximum_fusion.9), channel_id=1, source_target_pairs={{0,224},{32,0},{64,32},{96,64},{128,96},{160,128},{192,160},{224,1... | collective-permute-start | bytes 147464 | tf_op jit(solution)/shard_map/ppermute | solution.py:204
  90.4 26.9 %copy-start.1 = (bf16[32,96,256]{2,1,0:T(8,128)(2,1)S(1)}, bf16[32,96,256]{2,1,0:T(8,128)(2,1)}, u32[]{:S(2)}) copy-start(bf16[32,96,256]{2,1,0:T(8,128)(2,1)} %align_ref.3) | copy-start | bytes 4718596
  90.4 26.9 %copy-start.5 = (bf16[256,64]{0,1:T(8,128)(2,1)S(1)}, bf16[256,64]{0,1:T(8,128)(2,1)}, u32[]{:S(2)}) copy-start(bf16[256,64]{0,1:T(8,128)(2,1)} %param.6) | copy-start | bytes 98308
  90.4 10.7 %all-to-all-start.2 = ((bf16[8,32,768]{2,1,0:T(8,128)(2,1)}), bf16[8,32,768]{2,1,0:T(8,128)(2,1)S(1)}, u32[]{:S(2)}, u32[]{:S(2)}) async-start(bf16[8,32,768]{2,1,0:T(8,128)(2,1)} %broadcast_in_dim.4), calls=%async_computation.2 | async-start | bytes 786432 | tf_op jit(solution)/shard_map/all_to_all | solution.py:217
  94.3 4.1 %collective-permute-start.7 = (f32[24,128]{1,0:T(8,128)S(1)}, f32[24,128]{1,0:T(8,128)S(1)}, u32[]{:S(2)}, u32[]{:S(2)}) collective-permute-start(f32[24,128]{1,0:T(8,128)S(1)} %convert_reduce_fusion), channel_id=1, source_target_pairs={{0,2},{1,3},{2,0},{3,1},{4,6},{5,7},{6,4},{7,5},{8,10},{9,11},{10,... | collective-permute-start | bytes 36872 | tf_op jit(solution)/shard_map/ppermute | solution.py:204
  95.1 3.8 %collective-permute-start.8 = (f32[24,128]{1,0:T(8,128)S(1)}, f32[24,128]{1,0:T(8,128)S(1)}, u32[]{:S(2)}, u32[]{:S(2)}) collective-permute-start(f32[24,128]{1,0:T(8,128)S(1)} %convert_reduce_fusion), channel_id=1, source_target_pairs={{0,1},{1,2},{2,3},{3,0},{4,5},{5,6},{6,7},{7,4},{8,9},{9,10},{10,1... | collective-permute-start | bytes 36872 | tf_op jit(solution)/shard_map/ppermute | solution.py:204
  95.6 3.2 %collective-permute-start.9 = (f32[24,128]{1,0:T(8,128)S(1)}, f32[24,128]{1,0:T(8,128)S(1)}, u32[]{:S(2)}, u32[]{:S(2)}) collective-permute-start(f32[24,128]{1,0:T(8,128)S(1)} %convert_reduce_fusion), channel_id=1, source_target_pairs={{0,3},{1,0},{2,1},{3,2},{4,7},{5,4},{6,5},{7,6},{8,11},{9,8},{10,9... | collective-permute-start | bytes 36872 | tf_op jit(solution)/shard_map/ppermute | solution.py:204
  101.8 25.7 %all-to-all-start.3 = ((bf16[64,16,128]{2,1,0:T(8,128)(2,1)}), bf16[64,16,128]{2,1,0:T(8,128)(2,1)S(1)}, u32[]{:S(2)}, u32[]{:S(2)}) async-start(bf16[64,16,128]{2,1,0:T(8,128)(2,1)} %broadcast_in_dim.5), calls=%async_computation.3 | async-start | bytes 524288 | tf_op jit(solution)/shard_map/all_to_all | solution.py:217
